TPU v7x, 32 devices: a whole 2x2x4 slice. The times are simulated.
32 devices in a mesh: rad: 8 (over y, x, core), az: 4 (over z).
Axes of the slice: x: 2, y: 2, z: 4, core: 2. Of those that a mesh axis runs over, the one named last changes fastest.
Arguments:
- surface_mass: float32 [256, 16384], P('rad', 'az'), may hold values from 0.5 to 2
- outward_drift: float32 [256, 16384], P('rad', 'az'), may hold values from -1.2 to 1.2
- leftover_angular_drift: float32 [256, 16384], P('rad', 'az'), may hold values from -1.2 to 1.2
- angular_offsets: int32 [256], P('rad'), may hold values from 0 to 16383
- planetesimal_loop_number: int32 [32], replicated, may hold values from 0 to 255
- planetesimal_angle_bin: int32 [32], replicated, may hold values from 0 to 16383
- planetesimal_weights: float32 [32], replicated, may hold values from 0.001 to 0.01
Outputs:
- transported_density: float32 [256, 16384], P('rad', 'az')
- kicked_radial_velocity: float32 [256, 16384], P('rad', 'az')
- kicked_azimuthal_velocity: float32 [256, 16384], P('rad', 'az')
- embryo_disk_acceleration: float32 [2, 32], replicated
All inputs are finite; a program needn't handle non-finite values.
Results may differ from a plain program's by a relative error of at most 0.0003.
Values sent between devices are 32-bit elements; how exact they have to be, the bound alone decides.
A program may use at most 64 MiB of HBM per device.

v0:
```python
import jax
import jax.numpy as jnp
from jax import lax
from jax.sharding import PartitionSpec as P

ANGULAR_BINS = 16384
MODES = 256


gravity = 1.0
timestep_length = 0.05
courant = 0.4
softening = 0.02


def extended(block, sides, width, periodic):
    for axis, dim in sides:
        count = lax.axis_size(axis)
        forward = [(i, i + 1) for i in range(count - 1)]
        if periodic:
            forward.append((count - 1, 0))
        backward = [(target, source) for source, target in forward]
        low = lax.ppermute(
            lax.slice_in_dim(block, block.shape[dim] - width, None, axis=dim), axis, forward
        )
        high = lax.ppermute(lax.slice_in_dim(block, 0, width, axis=dim), axis, backward)
        block = jnp.concatenate([low, block, high], axis=dim)
    return block


def mode_tables(first, count):
    columns = first + jnp.arange(count, dtype=jnp.int32)
    orders = jnp.arange(MODES, dtype=jnp.int32)
    phases = orders[:, None] * (2 * columns[None, :] + 1) % (2 * ANGULAR_BINS)
    angles = phases.astype(jnp.float32) * (jnp.pi / ANGULAR_BINS)
    return jnp.concatenate([jnp.cos(angles), jnp.sin(angles)], axis=0)


def column_angles(first, count):
    columns = first + jnp.arange(count, dtype=jnp.int32)
    return (2 * columns + 1).astype(jnp.float32) * (jnp.pi / ANGULAR_BINS)


def cycle_radius(first, count, cell_step):
    cycles = first + jnp.arange(count, dtype=jnp.int32)
    return jnp.exp((cycles.astype(jnp.float32) + 0.5) * cell_step)


def donor_flux(orbital_speeds, upstream, downstream):
    return jnp.where(orbital_speeds > 0, orbital_speeds * upstream, orbital_speeds * downstream)


def rotate_cycles(block, angular_offsets, sections):
    for bit_place in range(sections):
        chosen = (angular_offsets >> bit_place & 1)[None, :, None] == 1
        block = jnp.where(chosen, jnp.roll(block, 2**bit_place, axis=2), block)
    return block


def on_device(
    surface_mass,
    outward_drift,
    leftover_angular_drift,
    angular_offsets,
    planetesimal_loop_number,
    planetesimal_angle_bin,
    planetesimal_weights,
):
    cycle_count, sector = surface_mass.shape
    cycle_total = lax.axis_size("rad") * cycle_count
    cycle_first = lax.axis_index("rad") * cycle_count
    column_first = lax.axis_index("az") * sector
    cell_step = 2.0 * jnp.pi / ANGULAR_BINS
    highest = lax.Precision.HIGHEST
    piled_quantities = jnp.stack([surface_mass, outward_drift, leftover_angular_drift])
    gathered = lax.all_gather(piled_quantities, "az", axis=2, tiled=True)
    whole_sections = (gathered.shape[2] - 1).bit_length()
    rotated = rotate_cycles(gathered, angular_offsets, whole_sections)
    moved_density = lax.dynamic_slice_in_dim(rotated, column_first, sector, 2)
    single_density, single_radial_velocity, lone_angular_drift = (
        moved_density[0],
        moved_density[1],
        moved_density[2],
    )
    density_with_halo = extended(
        jnp.stack([single_density, lone_angular_drift]), (("az", 2),), 1, True
    )
    orbital_speeds = 0.5 * (density_with_halo[1, :, :-1] + density_with_halo[1, :, 1:])
    fluxes = donor_flux(orbital_speeds, density_with_halo[0, :, :-1], density_with_halo[0, :, 1:])
    dens_two = single_density - courant * (fluxes[:, 1:] - fluxes[:, :-1])
    density_with_halo = extended(
        jnp.stack([dens_two, single_radial_velocity]), (("rad", 1),), 1, False
    )
    orbital_speeds = 0.5 * (density_with_halo[1, :-1] + density_with_halo[1, 1:])
    lower_cycle = cycle_first - 1 + jnp.arange(cycle_count + 1, dtype=jnp.int32)
    inside = (lower_cycle >= 0) & (lower_cycle <= cycle_total - 2)
    fluxes = jnp.where(
        inside[:, None],
        donor_flux(orbital_speeds, density_with_halo[0, :-1], density_with_halo[0, 1:]),
        0.0,
    )
    transported_density = dens_two - courant * (fluxes[1:] - fluxes[:-1])
    tables = mode_tables(column_first, sector)
    partial_value = (
        jnp.einsum("rc,mc->rm", transported_density, tables, precision=highest) * cell_step
    )
    spectra = lax.psum(partial_value, "az")
    folded = spectra.reshape(cycle_count, 2, MODES)
    decays = (jnp.arange(MODES, dtype=jnp.float32) + 0.5) * cell_step
    local_cycles = jnp.arange(cycle_count, dtype=jnp.int32)
    cycle_gap = local_cycles[:, None] - local_cycles[None, :]
    lower_kernel = jnp.where(
        cycle_gap[:, :, None] >= 0,
        jnp.exp(-decays * jnp.maximum(cycle_gap, 0).astype(jnp.float32)[:, :, None]),
        0.0,
    )
    upper_kernel = jnp.where(
        cycle_gap[:, :, None] <= 0,
        jnp.exp(-decays * jnp.maximum(-cycle_gap, 0).astype(jnp.float32)[:, :, None]),
        0.0,
    )
    lower_sum = jnp.einsum("ikm,kcm->icm", lower_kernel, folded, precision=highest)
    upper_sum = jnp.einsum("ikm,kcm->icm", upper_kernel, folded, precision=highest)
    up_moment = lower_sum[-1]
    down_moment = upper_sum[0]
    moments = jnp.stack([up_moment, down_moment])[None]
    every = lax.all_gather(moments, "rad", axis=0, tiled=True)
    own_index = lax.axis_index("rad")
    others = jnp.arange(every.shape[0], dtype=jnp.int32)
    below_gap = own_index - 1 - others
    above_gap = others - own_index - 1
    block_rate = (decays * cycle_count)[None, :]
    below_weight = jnp.where(
        below_gap[:, None] >= 0,
        jnp.exp(-block_rate * jnp.maximum(below_gap, 0).astype(jnp.float32)[:, None]),
        0.0,
    )
    above_weight = jnp.where(
        above_gap[:, None] >= 0,
        jnp.exp(-block_rate * jnp.maximum(above_gap, 0).astype(jnp.float32)[:, None]),
        0.0,
    )
    from_lower = jnp.einsum("dm,dcm->cm", below_weight, every[:, 0], precision=highest)
    from_upper = jnp.einsum("dm,dcm->cm", above_weight, every[:, 1], precision=highest)
    cycle_float = local_cycles.astype(jnp.float32)
    lift_up = jnp.exp(-decays[None, :] * (cycle_float + 1.0)[:, None])
    drop_down = jnp.exp(-decays[None, :] * (cycle_count - cycle_float)[:, None])
    lower_sum = lower_sum + lift_up[:, None, :] * from_lower[None]
    upper_sum = upper_sum + drop_down[:, None, :] * from_upper[None]
    decays_both = jnp.concatenate([decays, decays])
    lower_flat = lower_sum.reshape(cycle_count, 2 * MODES)
    upper_flat = upper_sum.reshape(cycle_count, 2 * MODES)
    even_part = decays_both * (lower_flat + upper_flat - spectra)
    odd_part = decays_both * (lower_flat - upper_flat)
    orders = jnp.arange(MODES, dtype=jnp.float32)
    doubled = jnp.where(orders > 0, 2.0, 1.0)
    radial_weight = jnp.concatenate([doubled * decays, doubled * decays])
    azim_weight = jnp.concatenate([doubled * orders, -doubled * orders])
    radial_coef = odd_part * radial_weight
    azim_coef = jnp.concatenate([even_part[:, MODES:], even_part[:, :MODES]], axis=1) * azim_weight
    radius = cycle_radius(cycle_first, cycle_count, cell_step)
    radial_disk = (
        -(gravity / cell_step) / radius[:, None] * jnp.dot(radial_coef, tables, precision=highest)
    )
    azimuthal_disk_pull = gravity / radius[:, None] * jnp.dot(azim_coef, tables, precision=highest)
    cell_angles = column_angles(column_first, sector)
    cos_cell = jnp.cos(cell_angles)[None, None, :]
    sin_cell = jnp.sin(cell_angles)[None, None, :]
    embryo_angles = (2 * planetesimal_angle_bin + 1).astype(jnp.float32) * (jnp.pi / ANGULAR_BINS)
    embryo_radii = jnp.exp((planetesimal_loop_number.astype(jnp.float32) + 0.5) * cell_step)
    embryo_cosines = jnp.cos(embryo_angles)
    embryo_sines = jnp.sin(embryo_angles)
    column_radius = radius[None, :, None]
    area = (radius * radius * cell_step * cell_step)[None, :, None]
    radial_emb = jnp.zeros_like(transported_density)
    azimuthal_embryo_pull = jnp.zeros_like(transported_density)
    pushes_x = []
    pushes_y = []
    block_size = 8
    for block in range(planetesimal_weights.shape[0] // block_size):
        first = block * block_size
        embryo_radius = embryo_radii[first : first + block_size][:, None, None]
        embryo_cos = embryo_cosines[first : first + block_size][:, None, None]
        embryo_sin = embryo_sines[first : first + block_size][:, None, None]
        embryo_weight = planetesimal_weights[first : first + block_size][:, None, None]
        cos_gap = cos_cell * embryo_cos + sin_cell * embryo_sin
        sin_gap = sin_cell * embryo_cos - cos_cell * embryo_sin
        squared = (
            column_radius * column_radius
            + embryo_radius * embryo_radius
            - 2.0 * column_radius * embryo_radius * cos_gap
            + softening * embryo_radius * (softening * embryo_radius)
        )
        inverse = lax.rsqrt(squared)
        cubed = inverse * inverse * inverse
        pulled = embryo_weight * cubed
        radial_emb = radial_emb - jnp.sum(
            pulled * (column_radius - embryo_radius * cos_gap), axis=0
        )
        azimuthal_embryo_pull = azimuthal_embryo_pull - jnp.sum(
            pulled * embryo_radius * sin_gap, axis=0
        )
        weighted = transported_density[None] * area * cubed
        pushes_x.append(
            jnp.sum(weighted * (column_radius * cos_cell - embryo_radius * embryo_cos), axis=(1, 2))
        )
        pushes_y.append(
            jnp.sum(weighted * (column_radius * sin_cell - embryo_radius * embryo_sin), axis=(1, 2))
        )
    partial_push = jnp.stack([jnp.concatenate(pushes_x), jnp.concatenate(pushes_y)])
    embryo_disk_acceleration = lax.psum(partial_push, ("rad", "az"))
    kicked_radial_velocity = single_radial_velocity + timestep_length * (radial_disk + radial_emb)
    kicked_azimuthal_velocity = lone_angular_drift + timestep_length * (
        azimuthal_disk_pull + azimuthal_embryo_pull
    )
    return (
        transported_density,
        kicked_radial_velocity,
        kicked_azimuthal_velocity,
        embryo_disk_acceleration,
    )


def solution(mesh):
    placed = (P("rad", "az"), P("rad", "az"), P("rad", "az"), P("rad"), P(), P(), P())
    return jax.shard_map(
        on_device,
        mesh=mesh,
        in_specs=placed,
        out_specs=(P("rad", "az"), P("rad", "az"), P("rad", "az"), P()),
        check_vma=False,
    )
```

profile of v0, /device:TPU:0, one launch (start us, length us, event | category | flops | bytes accessed | tf_op | source)
XLA Modules:
  0.0 328.1 jit_solution(4074819335090835696)
XLA Ops:
  7.3 2.6 pad_maximum_fusion.20
  19.3 3.4 %multiply_reduce_fusion.9 = (f32[32,4096]{1,0:T(8,128)}, f32[32,4096]{1,0:T(8,128)}) fusion(f32[8,4096]{1,0:T(8,128)S(1)} %get-tuple-element.56, f32[8]{0:T(128)S(1)} %get-tuple-element.87, f32[8]{0:T(128)S(1)} %get-tuple-element.83, f32[8,4096]{1,0:T(8,128)S(1)} %get-tuple-element.55, f32[8,32]{1,0:T(8,128)S(1)} %get-tuple-element.106, ...), kind=kLoop, calls=%fused_computation.46 | loop fusion | flops 12320768 | bytes 1444064 | tf_op jit(solution)/shard_map/reduce_sum | solution.py:200
  22.7 6.4 %multiply_reduce_fusion.11 = (f32[32,4096]{1,0:T(8,128)}, f32[32,4096]{1,0:T(8,128)}, f32[32,4096]{1,0:T(8,128)}, f32[32,4096]{1,0:T(8,128)}) fusion(f32[8,4096]{1,0:T(8,128)S(1)} %get-tuple-element.42, f32[8]{0:T(128)S(1)} %get-tuple-element.89, f32[8]{0:T(128)S(1)} %get-tuple-element.79, f32[8,4096]{1,0:T(8,128)S(1)} %get-tuple-element.43, ...), kind=kLoop, calls=%fused_computation.48 | loop fusion | flops 24641536 | bytes 2888000 | tf_op jit(solution)/shard_map/reduce_sum | solution.py:200
  30.3 17.9 %fusion.40 = (f32[256,4096]{1,0:T(8,128)}, f32[256,4096]{1,0:T(8,128)}) fusion(s32[4096]{0:T(1024)S(1)} %multiply_add_fusion.6), kind=kLoop, calls=%fused_computation.79 | loop fusion | flops 14680064 | bytes 8404992 | tf_op jit(solution)/shard_map/cos | solution.py:36
  48.2 79.9 %all-gather.3.cloned.1.call-done = f32[3,32,16384]{2,1,0:T(8,128)} async-done(((f32[3,32,4096]{2,1,0:T(8,128)}), f32[3,32,16384]{2,1,0:T(8,128)}) %all-gather.3.cloned.1.call-update) | async-done | bytes 6291472 | tf_op jit(solution)/shard_map/all_gather | solution.py:76
  129.0 6.3 %maximum_select_fusion = f32[3,32,16384]{2,1,0:T(8,128)S(1)} fusion(f32[3,32,16384]{2,1,0:T(8,128)} %all-gather.3.cloned.1.call-done, f32[3,32,16383]{2,1,0:T(8,128)} %bitcast.75, f32[3,32,1]{2,1,0:T(8,128)S(1)} %slice.312, pred[32]{0:T(512)(128)(4,1)S(1)} %get-tuple-element.128), kind=kLoop, calls=%fused_computation.1 | loop fusion | flops 3145728 | bytes 18874400 | tf_op jit(solution)/shard_map/jit(_where)/select_n | solution.py:56
  144.2 1.9 maximum_select_fusion.6
  146.2 3.1 slice.327
  149.2 3.8 %maximum_select_fusion.7 = f32[3,32,16384]{2,1,0:T(8,128)S(1)} fusion(f32[3,32,16384]{2,1,0:T(8,128)S(1)} %maximum_select_fusion.6, f32[3,32,16256]{2,1,0:T(8,128)} %slice.327, f32[3,32,128]{2,1,0:T(8,128)S(1)} %slice.326, pred[32]{0:T(512)(128)(4,1)S(1)} %get-tuple-element.122), kind=kLoop, calls=%fused_computation.8 | loop fusion | flops 3145728 | bytes 18874400 | tf_op jit(solution)/shard_map/jit(_where)/select_n | solution.py:56
  153.0 3.1 slice.329
  156.1 3.8 %maximum_select_fusion.8 = f32[3,32,16384]{2,1,0:T(8,128)S(1)} fusion(f32[3,32,16384]{2,1,0:T(8,128)S(1)} %maximum_select_fusion.7, f32[3,32,16128]{2,1,0:T(8,128)} %slice.329, f32[3,32,256]{2,1,0:T(8,128)S(1)} %slice.328, pred[32]{0:T(512)(128)(4,1)S(1)} %get-tuple-element.123), kind=kLoop, calls=%fused_computation.9 | loop fusion | flops 3145728 | bytes 18874400 | tf_op jit(solution)/shard_map/jit(_where)/select_n | solution.py:56
  159.9 3.0 slice.331
  162.9 3.7 %maximum_select_fusion.9 = f32[3,32,16384]{2,1,0:T(8,128)S(1)} fusion(f32[3,32,16384]{2,1,0:T(8,128)S(1)} %maximum_select_fusion.8, f32[3,32,15872]{2,1,0:T(8,128)} %slice.331, f32[3,32,512]{2,1,0:T(8,128)S(1)} %slice.330, pred[32]{0:T(512)(128)(4,1)S(1)} %get-tuple-element.124), kind=kLoop, calls=%fused_computation.10 | loop fusion | flops 3145728 | bytes 18874400 | tf_op jit(solution)/shard_map/jit(_where)/select_n | solution.py:56
  166.6 3.0 slice.333
  169.6 3.7 %maximum_select_fusion.10 = f32[3,32,16384]{2,1,0:T(8,128)S(1)} fusion(f32[3,32,16384]{2,1,0:T(8,128)S(1)} %maximum_select_fusion.9, f32[3,32,15360]{2,1,0:T(8,128)} %slice.333, f32[3,32,1024]{2,1,0:T(8,128)S(1)} %slice.332, pred[32]{0:T(512)(128)(4,1)S(1)} %get-tuple-element.125), kind=kLoop, calls=%fused_computation.11 | loop fusion | flops 3145728 | bytes 18874400 | tf_op jit(solution)/shard_map/jit(_where)/select_n | solution.py:56
  173.3 2.8 slice.335
  176.1 3.5 %maximum_select_fusion.11 = f32[3,32,16384]{2,1,0:T(8,128)S(1)} fusion(f32[3,32,16384]{2,1,0:T(8,128)S(1)} %maximum_select_fusion.10, f32[3,32,14336]{2,1,0:T(8,128)} %slice.335, f32[3,32,2048]{2,1,0:T(8,128)S(1)} %slice.334, pred[32]{0:T(512)(128)(4,1)S(1)} %get-tuple-element.126), kind=kLoop, calls=%fused_computation.12 | loop fusion | flops 3145728 | bytes 18874400 | tf_op jit(solution)/shard_map/jit(_where)/select_n | solution.py:56
  180.1 3.4 %maximum_select_fusion.12 = f32[3,32,16384]{2,1,0:T(8,128)} fusion(f32[3,32,16384]{2,1,0:T(8,128)S(1)} %maximum_select_fusion.11, f32[3,32,12288]{2,1,0:T(8,128)S(1)} %slice.337, f32[3,32,4096]{2,1,0:T(8,128)S(1)} %slice.336, pred[32]{0:T(512)(128)(4,1)S(1)} %get-tuple-element.127), kind=kLoop, calls=%fused_computation.13 | loop fusion | flops 3145728 | bytes 18874400 | tf_op jit(solution)/shard_map/jit(_where)/select_n | solution.py:56
  183.5 3.2 fusion.85
  186.8 1.8 fusion.44
  189.4 3.8 %collective-permute-start.1 = (f32[2,32,1]{2,1,0:T(8,128)}, f32[2,32,1]{2,1,0:T(8,128)}, u32[]{:S(2)}, u32[]{:S(2)}) collective-permute-start(f32[2,32,1]{2,1,0:T(8,128)} %get-tuple-element.36), channel_id=1, source_target_pairs={{1,0},{2,1},{3,2},{0,3},{5,4},{6,5},{7,6},{4,7},{9,8},{10,9},{11,1... | collective-permute-start | bytes 776 | tf_op jit(solution)/shard_map/ppermute | solution.py:26
  199.9 3.2 collective-permute-done.3
  207.0 8.4 %fusion.45 = f32[32,512]{1,0:T(8,128)} fusion(f32[32,4096]{1,0:T(8,128)S(1)} %get-tuple-element.23, f32[256,4096]{1,0:T(8,128)S(1)} %copy-done.2, f32[256,4096]{1,0:T(8,128)S(1)} %copy-done), kind=kOutput, calls=%fused_computation.87 | convolution fusion | flops 807419904 | bytes 8978432 | tf_op jit(solution)/shard_map/rc,mc->rm/dot_general | solution.py:105
  215.6 6.4 %multiply_reduce_fusion.7 = (f32[8]{0:T(128)S(1)}, f32[8]{0:T(128)S(1)}, f32[8]{0:T(128)S(1)}) fusion(f32[8]{0:T(128)} %get-tuple-element.67, f32[32,4096]{1,0:T(8,128)S(1)} %copy-done.6, f32[32,4096]{1,0:T(8,128)} %get-tuple-element.22, f32[8]{0:T(128)} %copy-done.50, f32[8,4096]{1,0:T(8,128)} %copy-done.15, f32[8,32]{1,0:T(8,128)} %copy-done.27, ...), kind=kLoop, calls=%fused_computation.44 | loop fusion | flops 28311528 | bytes 1448224 | tf_op jit(solution)/shard_map/reduce_sum | solution.py:205
  222.2 4.5 %multiply_reduce_fusion.3 = (f32[8]{0:T(128)S(1)}, f32[8]{0:T(128)S(1)}, f32[8]{0:T(128)S(1)}) fusion(f32[8]{0:T(128)S(1)} %copy-done.48, f32[32,4096]{1,0:T(8,128)S(1)} %copy-done.5, f32[32,4096]{1,0:T(8,128)S(1)} %copy-done.8, f32[8]{0:T(128)S(1)} %copy-done.51, f32[8,4096]{1,0:T(8,128)S(1)} %copy-done.16, f32[8,32]{1,0:T(8,128)S(1)} %copy-done.28, ...), kind=kLoop, calls=%fused_computation.40 | loop fusion | flops 28311528 | bytes 1448224 | tf_op jit(solution)/shard_map/reduce_sum | solution.py:208
  226.7 3.8 %multiply_reduce_fusion.4 = (f32[8]{0:T(128)S(1)}, f32[8]{0:T(128)S(1)}, f32[32,4096]{1,0:T(8,128)S(1)}, f32[32,4096]{1,0:T(8,128)S(1)}) fusion(f32[8]{0:T(128)S(1)} %copy-done.42, f32[32,4096]{1,0:T(8,128)S(1)} %copy-done.7, f32[32,4096]{1,0:T(8,128)S(1)} %copy-done.9, f32[8]{0:T(128)S(1)} %copy-done.43, f32[8,4096]{1,0:T(8,128)S(1)} %get-tuple-element.61, ...), kind=kLoop, calls=%fused_computation.41 | loop fusion | flops 19660784 | bytes 3017056 | tf_op jit(solution)/shard_map/reduce_sum | solution.py:205
  230.7 42.3 %psum.15 = f32[2,32]{1,0:T(2,128)} all-reduce(f32[2,32]{1,0:T(2,128)S(1)} %pad_maximum_fusion.33), channel_id=1, replica_groups=mesh['rad'=8,'az'=4] {'rad','az'}, use_global_device_ids=true, to_apply=%region_17.18 | all-reduce | flops 64 | bytes 512 | tf_op jit(solution)/shard_map/psum | solution.py:211
  274.1 8.3 %fusion.26 = f32[256,2,32]{2,1,0:T(2,128)} fusion(f32[32,2,256]{0,1,2:T(2,128)S(1)} %copy.46, f32[32,32]{1,0:T(8,128)} %maximum_convert_fusion.1, f32[256]{0:T(256)} %copy-done.45, pred[32,32]{1,0:T(8,128)(4,1)} %fusion.67), kind=kOutput, calls=%fused_computation.65 | convolution fusion | flops 6815744 | bytes 137216 | tf_op jit(solution)/shard_map/ikm,kcm->icm/dot_general | solution.py:122
  284.1 8.4 %fusion.22 = f32[256,2,32]{2,1,0:T(2,128)} fusion(f32[32,2,256]{0,1,2:T(2,128)S(1)} %copy.46, f32[32,32]{1,0:T(8,128)} %maximum_convert_fusion, f32[256]{0:T(256)} %copy-done.45, pred[32,32]{1,0:T(8,128)(4,1)} %fusion.66), kind=kOutput, calls=%fused_computation.61 | convolution fusion | flops 6815744 | bytes 137216 | tf_op jit(solution)/shard_map/ikm,kcm->icm/dot_general | solution.py:123
  294.3 9.9 %all-gather = f32[16,2,256]{2,1,0:T(2,128)S(1)} all-gather(f32[2,2,256]{2,1,0:T(2,128)S(1)} %pad_maximum_fusion.29), channel_id=2, replica_groups=mesh['rad'=8,'az'=4] {'rad'}, dimensions={0}, use_global_device_ids=true | all-gather | bytes 36864 | tf_op jit(solution)/shard_map/all_gather | solution.py:127
  305.9 9.5 %fusion.10 = f32[32,4096]{1,0:T(8,128)} fusion(f32[256,4096]{1,0:T(8,128)} %get-tuple-element.65, f32[256,4096]{1,0:T(8,128)} %get-tuple-element.64, f32[32,4096]{1,0:T(8,128)S(1)} %get-tuple-element.20, f32[32,4096]{1,0:T(8,128)S(1)} %copy-done.13, f32[32,4096]{1,0:T(8,128)} %get-tuple-element.94, f32[32,4096]{1,0:T(8,128)} %get-tuple-element.13, ...), kind=kOutput, calls=%fused_computation.33 | convolution fusion | flops 808484864 | bytes 11604096 | tf_op jit(solution)/shard_map/dot_general | solution.py:163
  315.4 5.7 %fusion.7 = f32[32,4096]{1,0:T(8,128)} fusion(f32[256,4096]{1,0:T(8,128)S(1)} %copy-done.3, f32[256,4096]{1,0:T(8,128)S(1)} %copy-done.1, f32[32,4096]{1,0:T(8,128)S(1)} %get-tuple-element.21, f32[32,4096]{1,0:T(8,128)S(1)} %copy-done.10, f32[32,4096]{1,0:T(8,128)S(1)} %copy-done.12, f32[32,4096]{1,0:T(8,128)S(1)} %copy-done.11, f32[32]{0:T(128)S(1)} %copy-done.46, ...), kind=kOutput, calls=%fused_computation.30 | convolution fusion | flops 808484864 | bytes 11602048 | tf_op jit(solution)/shard_map/dot_general | solution.py:165
  (211 shorter events, 38.4 us)
Async XLA Ops:
  7.2 7.1 %copy-start.58 = (s32[32]{0:T(128)S(1)}, s32[32]{0:T(128)}, u32[]{:S(2)}) copy-start(s32[32]{0:T(128)} %param.11) | copy-start | bytes 388
  7.2 7.1 %copy-start.59 = (s32[32]{0:T(128)S(1)}, s32[32]{0:T(128)}, u32[]{:S(2)}) copy-start(s32[32]{0:T(128)} %param.12) | copy-start | bytes 388
  7.2 7.2 %copy-start.26 = (f32[32]{0:T(128)S(1)}, f32[32]{0:T(128)}, u32[]{:S(2)}) copy-start(f32[32]{0:T(128)} %param.13) | copy-start | bytes 388
  7.2 7.8 %copy-start.56 = (s32[32]{0:T(128)S(1)}, s32[32]{0:T(128)}, u32[]{:S(2)}) copy-start(s32[32]{0:T(128)} %param.10) | copy-start | bytes 388
  7.2 120.9 %all-gather.3.cloned.1.call-start = ((), (), s32[]{:S(2)}) async-start(), calls=%async_computation | async-start | bytes 7864320 | tf_op jit(solution)/shard_map/all_gather | solution.py:76
  9.9 263.2 %all-reduce.2.cloned.1.call-start = ((), (), s32[]{:S(2)}) async-start(), calls=%async_computation.1 | async-start | bytes 131072 | tf_op jit(solution)/shard_map/psum | solution.py:107
  10.5 19.8 %copy-start.39 = (f32[32]{0:T(128)}, f32[32]{0:T(128)S(1)}, u32[]{:S(2)}) copy-start(f32[32]{0:T(128)S(1)} %get-tuple-element.130) | copy-start | bytes 388
  10.5 19.7 %copy-start.45 = (f32[256]{0:T(256)}, f32[256]{0:T(256)S(1)}, u32[]{:S(2)}) copy-start(f32[256]{0:T(256)S(1)} %fusion.73) | copy-start | bytes 3076
  16.3 13.9 %copy-start.50 = (f32[8]{0:T(128)}, f32[8]{0:T(128)S(1)}, u32[]{:S(2)}) copy-start(f32[8]{0:T(128)S(1)} %get-tuple-element.79) | copy-start | bytes 100
  16.3 13.9 %copy-start.52 = (f32[8]{0:T(128)}, f32[8]{0:T(128)S(1)}, u32[]{:S(2)}) copy-start(f32[8]{0:T(128)S(1)} %get-tuple-element.81) | copy-start | bytes 100
  16.3 13.9 %copy-start.54 = (f32[8]{0:T(128)}, f32[8]{0:T(128)S(1)}, u32[]{:S(2)}) copy-start(f32[8]{0:T(128)S(1)} %get-tuple-element.83) | copy-start | bytes 100
  17.0 13.3 %copy-start.27 = (f32[8,32]{1,0:T(8,128)}, f32[8,32]{1,0:T(8,128)S(1)}, u32[]{:S(2)}) copy-start(f32[8,32]{1,0:T(8,128)S(1)} %get-tuple-element.104) | copy-start | bytes 3076
  17.0 13.3 %copy-start.29 = (f32[8,32]{1,0:T(8,128)}, f32[8,32]{1,0:T(8,128)S(1)}, u32[]{:S(2)}) copy-start(f32[8,32]{1,0:T(8,128)S(1)} %get-tuple-element.105) | copy-start | bytes 3076
  17.7 12.6 %copy-start.33 = (f32[8,32]{1,0:T(8,128)}, f32[8,32]{1,0:T(8,128)S(1)}, u32[]{:S(2)}) copy-start(f32[8,32]{1,0:T(8,128)S(1)} %get-tuple-element.100) | copy-start | bytes 3076
  17.7 12.6 %copy-start.37 = (f32[8,32]{1,0:T(8,128)}, f32[8,32]{1,0:T(8,128)S(1)}, u32[]{:S(2)}) copy-start(f32[8,32]{1,0:T(8,128)S(1)} %get-tuple-element.103) | copy-start | bytes 3076
  18.7 11.6 %copy-start.15 = (f32[8,4096]{1,0:T(8,128)}, f32[8,4096]{1,0:T(8,128)S(1)}, u32[]{:S(2)}) copy-start(f32[8,4096]{1,0:T(8,128)S(1)} %get-tuple-element.43) | copy-start | bytes 393220
  18.7 11.6 %copy-start.19 = (f32[8,4096]{1,0:T(8,128)}, f32[8,4096]{1,0:T(8,128)S(1)}, u32[]{:S(2)}) copy-start(f32[8,4096]{1,0:T(8,128)S(1)} %get-tuple-element.58) | copy-start | bytes 393220
  189.4 6.0 %collective-permute-start = (f32[2,32,1]{2,1,0:T(8,128)}, f32[2,32,1]{2,1,0:T(8,128)}, u32[]{:S(2)}, u32[]{:S(2)}) collective-permute-start(f32[2,32,1]{2,1,0:T(8,128)} %get-tuple-element.35), channel_id=1, source_target_pairs={{0,1},{1,2},{2,3},{3,0},{4,5},{5,6},{6,7},{7,4},{8,9},{9,10},{10,1... | collective-permute-start | bytes 776 | tf_op jit(solution)/shard_map/ppermute | solution.py:23
  189.4 6.0 %collective-permute-start.1 = (f32[2,32,1]{2,1,0:T(8,128)}, f32[2,32,1]{2,1,0:T(8,128)}, u32[]{:S(2)}, u32[]{:S(2)}) collective-permute-start(f32[2,32,1]{2,1,0:T(8,128)} %get-tuple-element.36), channel_id=1, source_target_pairs={{1,0},{2,1},{3,2},{0,3},{5,4},{6,5},{7,6},{4,7},{9,8},{10,9},{11,1... | collective-permute-start | bytes 776 | tf_op jit(solution)/shard_map/ppermute | solution.py:26
  197.0 2.9 collective-permute-start.2
  198.3 4.8 %collective-permute-start.3 = (f32[2,1,4096]{2,1,0:T(1,128)S(1)}, f32[2,1,4096]{2,1,0:T(1,128)S(1)}, u32[]{:S(2)}, u32[]{:S(2)}) collective-permute-start(f32[2,1,4096]{2,1,0:T(1,128)S(1)} %get-tuple-element.32), channel_id=1, source_target_pairs={{4,0},{8,4},{12,8},{16,12},{20,16},{24,20},{28,24},{5,1},{9,5},{13... | collective-permute-start | bytes 98312 | tf_op jit(solution)/shard_map/ppermute | solution.py:26
  204.6 10.8 %copy-start.4 = (f32[32,4096]{1,0:T(8,128)}, f32[32,4096]{1,0:T(8,128)S(1)}, u32[]{:S(2)}) copy-start(f32[32,4096]{1,0:T(8,128)S(1)} %get-tuple-element.23) | copy-start | bytes 1572868
  207.0 8.6 %copy-start.6 = (f32[32,4096]{1,0:T(8,128)S(1)}, f32[32,4096]{1,0:T(8,128)}, u32[]{:S(2)}) copy-start(f32[32,4096]{1,0:T(8,128)} %get-tuple-element.113) | copy-start | bytes 1572868
  274.1 31.0 %copy-start.14 = (f32[32,512]{1,0:T(8,128)S(1)}, f32[32,512]{1,0:T(8,128)}, u32[]{:S(2)}) copy-start(f32[32,512]{1,0:T(8,128)} %all-reduce.2.cloned.1.call-done) | copy-start | bytes 196612
  274.1 31.7 %copy-start.13 = (f32[32,4096]{1,0:T(8,128)S(1)}, f32[32,4096]{1,0:T(8,128)}, u32[]{:S(2)}) copy-start(f32[32,4096]{1,0:T(8,128)} %get-tuple-element.17) | copy-start | bytes 1572868
  305.8 9.5 %copy-start.1 = (f32[256,4096]{1,0:T(8,128)S(1)}, f32[256,4096]{1,0:T(8,128)}, u32[]{:S(2)}) copy-start(f32[256,4096]{1,0:T(8,128)} %get-tuple-element.64) | copy-start | bytes 12582916
  305.8 9.5 %copy-start.3 = (f32[256,4096]{1,0:T(8,128)S(1)}, f32[256,4096]{1,0:T(8,128)}, u32[]{:S(2)}) copy-start(f32[256,4096]{1,0:T(8,128)} %get-tuple-element.65) | copy-start | bytes 12582916
  305.8 9.5 %copy-start.10 = (f32[32,4096]{1,0:T(8,128)S(1)}, f32[32,4096]{1,0:T(8,128)}, u32[]{:S(2)}) copy-start(f32[32,4096]{1,0:T(8,128)} %get-tuple-element.16) | copy-start | bytes 1572868
  305.9 9.5 %copy-start.11 = (f32[32,4096]{1,0:T(8,128)S(1)}, f32[32,4096]{1,0:T(8,128)}, u32[]{:S(2)}) copy-start(f32[32,4096]{1,0:T(8,128)} %get-tuple-element.12) | copy-start | bytes 1572868
  305.9 9.5 %copy-start.12 = (f32[32,4096]{1,0:T(8,128)S(1)}, f32[32,4096]{1,0:T(8,128)}, u32[]{:S(2)}) copy-start(f32[32,4096]{1,0:T(8,128)} %get-tuple-element.95) | copy-start | bytes 1572868
  305.9 9.5 %copy-start.25 = (f32[512]{0:T(512)S(1)}, f32[512]{0:T(512)}, u32[]{:S(2)}) copy-start(f32[512]{0:T(512)} %pad_maximum_fusion.32) | copy-start | bytes 6148
  305.9 9.5 %copy-start.46 = (f32[32]{0:T(128)S(1)}, f32[32]{0:T(128)}, u32[]{:S(2)}) copy-start(f32[32]{0:T(128)} %get-tuple-element.134) | copy-start | bytes 388
  (34 other events, 190.7 us)
Sparse Core Ops, SparseCore 0:
  10.0 118.0 all-gather.2
  215.5 37.9 all-reduce.1
where the time goes:
time: 333 us; the launch traced here: 328 us
  other arithmetic  101 us (30%)
  waiting for transfers between devices  84.8 us (25%)
  blocking collectives  52.2 us (16%)
  matrix products  40.3 us (12%)
  local copies, waits for them, and re-layouts  27.7 us (8%)
  between operations  15.4 us (5%)
  starting transfers between devices  6.74 us (2%)
    all_gather x1, waiting for transfers between devices, on_device(): gathered = lax.all_gather(piled_quantities, 'az', axis=2, tiled=True)  79.9 us
    psum x1, blocking collectives, on_device(): embryo_disk_acceleration = lax.psum(partial_push, ('rad', 'az'))  42.3 us
    select_n x14, other arithmetic, rotate_cycles(): block = jnp.where(chosen, jnp.roll(block, 2 ** bit_place, axis=2), block)  40.3 us
    slice x20, local copies, waits for them, and re-layouts, rotate_cycles(): block = jnp.where(chosen, jnp.roll(block, 2 ** bit_place, axis=2), block)  20 us
    cos x1, other arithmetic, mode_tables(): return jnp.concatenate([jnp.cos(angles), jnp.sin(angles)], axis=0)  17.9 us
    reduce_sum x2, other arithmetic, on_device(): jnp.sum(weighted * (column_radius * cos_cell - embryo_radius * embryo_cos...  10.2 us
    all_gather x1, blocking collectives, on_device(): every = lax.all_gather(moments, 'rad', axis=0, tiled=True)  9.92 us
    reduce_sum x2, other arithmetic, on_device(): jnp.sum(pulled * embryo_radius * sin_gap, axis=0)  9.79 us
  transfers between devices with their start and end apart: 6, of which 3 were waited for; matrix products, arithmetic and copies ran while one was open for 16% of the time, Pallas kernels for 0%

commit v1 on v0

v1 whole, which is shorter than its diff:
```python
import jax
import jax.numpy as jnp
from jax import lax
from jax.experimental import pallas as pl
from jax.experimental.pallas import tpu as pltpu
from jax.sharding import PartitionSpec as P

ANGULAR_BINS = 16384
MODES = 256
LANES = 128

gravity = 1.0
timestep_length = 0.05
courant = 0.4
softening = 0.02

VMEM = pl.BlockSpec(memory_space=pltpu.VMEM)
SMEM = pl.BlockSpec(memory_space=pltpu.SMEM)
f32 = jnp.float32
bf16 = jnp.bfloat16


def call(body, outs, specs, scratch=(), flops=0):
    return pl.pallas_call(
        body,
        out_shape=outs,
        in_specs=specs,
        out_specs=jax.tree.map(lambda _: VMEM, outs),
        scratch_shapes=list(scratch),
        compiler_params=pltpu.CompilerParams(vmem_limit_bytes=48 * 1024 * 1024),
        cost_estimate=pl.CostEstimate(flops=flops, bytes_accessed=1 << 20, transcendentals=0),
    )


def gap(emb_ref, e, count, half_cos_ref, half_sin_ref):
    s = half_sin_ref[...] * emb_ref[3 * count + e] - half_cos_ref[...] * emb_ref[4 * count + e]
    return 2.0 * emb_ref[e] * (s * s)


def embryo_field(
    a_ref, b_ref, r_ref, emb_ref, cos_ref, sin_ref, hc_ref, hs_ref, rad_ref, azi_ref, p_ref, q_ref, k_ref
):
    count = p_ref.shape[0]

    def prepare(e, _):
        radius, cos_e, sin_e = emb_ref[e], emb_ref[count + e], emb_ref[2 * count + e]
        p_ref[e] = radius * (cos_ref[...] * cos_e + sin_ref[...] * sin_e)
        q_ref[e] = radius * (sin_ref[...] * cos_e - cos_ref[...] * sin_e)
        k_ref[e] = gap(emb_ref, e, count, hc_ref, hs_ref)
        return 0

    lax.fori_loop(0, count, prepare, 0)

    def row(i, _):
        def one(e, sums):
            s0, s1, s2 = sums
            p, q = p_ref[e], q_ref[e]
            inverse = lax.rsqrt(a_ref[i * count + e] + b_ref[i * count + e] * k_ref[e])
            t = inverse * inverse * inverse
            return s0 + t, s1 + t * p, s2 + t * q

        zero = jnp.zeros(p_ref.shape[1:], f32)
        s0, s1, s2 = lax.fori_loop(0, count, one, (zero, zero, zero), unroll=8)
        rad_ref[i] = s1 - r_ref[i] * s0
        azi_ref[i] = -s2
        return 0

    lax.fori_loop(0, rad_ref.shape[0], row, 0)


def shift_cycles(start_ref, g_ref, dens_ref, vrad_ref, vphi_ref, line_ref):
    rows, blocks = dens_ref.shape[:2]
    whole = g_ref.shape[2]
    total = whole * LANES
    extra = line_ref.shape[1] - whole
    lane = lax.broadcasted_iota(jnp.int32, (blocks, LANES), 1)

    def window(field, start):
        block = start // LANES
        rest = start % LANES
        first = pltpu.roll(line_ref[field, pl.ds(block, blocks), :], LANES - rest, 1)
        second = pltpu.roll(line_ref[field, pl.ds(block + 1, blocks), :], LANES - rest, 1)
        return jnp.where(lane < LANES - rest, first, second)

    def row(i, _):
        for field in range(3):
            line_ref[field, :whole] = g_ref[field, i]
            line_ref[field, whole:] = g_ref[field, i, :extra]
        here = start_ref[i]
        below = (here + total - 1) % total
        above = (here + 1) % total
        d, dm, dp = window(0, here), window(0, below), window(0, above)
        v, vm, vp = window(2, here), window(2, below), window(2, above)
        w = 0.5 * (v + vp)
        flux = w * jnp.where(w > 0, d, dp)
        w = 0.5 * (vm + v)
        flux_below = w * jnp.where(w > 0, dm, d)
        dens_ref[i] = d - courant * (flux - flux_below)
        vrad_ref[i] = window(1, here)
        vphi_ref[i] = v
        return 0

    lax.fori_loop(0, rows, row, 0)


def split(x):
    high = x.astype(bf16)
    return high, (x - high.astype(f32)).astype(bf16)


def split_outside(x):
    high = lax.reduce_precision(x, 8, 7)
    return high.astype(bf16), (x - high).astype(bf16)


def dot3(ah, al, bh, bl):
    def dot(a, b):
        return jnp.dot(a, b, preferred_element_type=f32)

    return dot(ah, bh) + (dot(al, bh) + dot(ah, bl))


def transport(
    edge_ref, d_ref, v_ref, low_ref, high_ref, th_ref, tl_ref, ct_ref, st_ref, out_ref, spec_ref, g_ref
):
    rows, blocks = d_ref.shape[:2]

    def face(da, va, db, vb):
        u = 0.5 * (va + vb)
        return u * jnp.where(u > 0, da, db)

    bottom = jnp.where(edge_ref[0] == 0, face(low_ref[0, 0], low_ref[1, 0], d_ref[0], v_ref[0]), 0.0)
    top = jnp.where(
        edge_ref[1] == 0, face(d_ref[rows - 1], v_ref[rows - 1], high_ref[0, 0], high_ref[1, 0]), 0.0
    )

    def row(i, below):
        flux = face(d_ref[i], v_ref[i], d_ref[i + 1], v_ref[i + 1])
        out_ref[i] = d_ref[i] - courant * (flux - below)
        return flux

    below = lax.fori_loop(0, rows - 1, row, bottom, unroll=4)
    out_ref[rows - 1] = d_ref[rows - 1] - courant * (top - below)

    chunk = 8

    def modes(c, _):
        x = out_ref[pl.ds(c * chunk, chunk)].reshape(chunk * blocks, LANES)
        high, low = split(x)
        g_ref[...] = dot3(high, low, th_ref[...], tl_ref[...])
        for k in range(chunk):
            gc = g_ref[k * blocks : (k + 1) * blocks, :MODES]
            gs = g_ref[k * blocks : (k + 1) * blocks, MODES:]
            ct, st = ct_ref[...], st_ref[...]
            spec_ref[pl.ds(c * chunk + k, 1), :MODES] = jnp.sum(ct * gc - st * gs, 0, keepdims=True)
            spec_ref[pl.ds(c * chunk + k, 1), MODES:] = jnp.sum(st * gc + ct * gs, 0, keepdims=True)
        return 0

    lax.fori_loop(0, rows // chunk, modes, 0)


def embryo_push(
    a_ref, b_ref, r_ref, area_ref, emb_ref, d_ref, cos_ref, sin_ref, hc_ref, hs_ref, x_ref, y_ref, m_ref
):
    rows = d_ref.shape[0]
    count = x_ref.shape[0]

    def weigh(i, _):
        m_ref[i] = d_ref[i] * area_ref[i]
        return 0

    lax.fori_loop(0, rows, weigh, 0, unroll=4)

    def embryo(e, _):
        radius, cos_e, sin_e = emb_ref[e], emb_ref[count + e], emb_ref[2 * count + e]
        cosine, sine = cos_ref[...], sin_ref[...]
        p = gap(emb_ref, e, count, hc_ref, hs_ref)
        base_x, base_y = radius * cos_e, radius * sin_e

        def row(i, sums):
            inverse = lax.rsqrt(a_ref[i * count + e] + b_ref[i * count + e] * p)
            t = inverse * inverse * inverse * m_ref[i]
            return (
                sums[0] + t * (r_ref[i] * cosine - base_x),
                sums[1] + t * (r_ref[i] * sine - base_y),
            )

        zero = jnp.zeros(p.shape, f32)
        x, y = lax.fori_loop(0, rows, row, (zero, zero), unroll=8)
        x_ref[pl.ds(e, 1), :] = jnp.sum(x, 0, keepdims=True)
        y_ref[pl.ds(e, 1), :] = jnp.sum(y, 0, keepdims=True)
        return 0

    lax.fori_loop(0, count, embryo, 0)


def kick(
    r_ref, x_ref, from_ref, rate_ref, ct_ref, st_ref, th_ref, tl_ref, vr_ref, vp_ref, er_ref, ep_ref,
    outr_ref, outp_ref, low_ref, up_ref, zrh_ref, zrl_ref, zph_ref, zpl_ref,
):
    rows, blocks = vr_ref.shape[:2]
    decay, factor = rate_ref[0:1], rate_ref[1:2]
    rweight, aweight = rate_ref[2:3], rate_ref[3:4]

    def sweep(i, carried):
        low, up = carried
        j = rows - 1 - i
        low = x_ref[pl.ds(i, 1), :] + factor * low
        up = x_ref[pl.ds(j, 1), :] + factor * up
        low_ref[pl.ds(i, 1), :] = low
        up_ref[pl.ds(j, 1), :] = up
        return low, up

    lax.fori_loop(0, rows, sweep, (from_ref[0:1], from_ref[1:2]), unroll=4)
    even = decay * (low_ref[...] + up_ref[...] - x_ref[...])
    odd = decay * (low_ref[...] - up_ref[...])
    low_ref[...] = odd * rweight
    up_ref[...] = jnp.concatenate([even[:, MODES:], even[:, :MODES]], axis=1) * aweight

    def twist(i, _):
        ct, st = ct_ref[...], st_ref[...]
        where = pl.ds(pl.multiple_of(i * blocks, blocks), blocks)
        for src, high_ref, low_out in ((low_ref, zrh_ref, zrl_ref), (up_ref, zph_ref, zpl_ref)):
            cc, cs = src[pl.ds(i, 1), :MODES], src[pl.ds(i, 1), MODES:]
            high_ref[where, :MODES], low_out[where, :MODES] = split(cc * ct + cs * st)
            high_ref[where, MODES:], low_out[where, MODES:] = split(cs * ct - cc * st)
        return 0

    lax.fori_loop(0, rows, twist, 0)
    chunk = 8

    def synth(c, _):
        where = pl.ds(pl.multiple_of(c * chunk * blocks, chunk * blocks), chunk * blocks)
        shape = (chunk, blocks, LANES)
        r = dot3(zrh_ref[where], zrl_ref[where], th_ref[...], tl_ref[...]).reshape(shape)
        p = dot3(zph_ref[where], zpl_ref[where], th_ref[...], tl_ref[...]).reshape(shape)
        for k in range(chunk):
            i = c * chunk + k
            scale = gravity / r_ref[i]
            outr_ref[i] = vr_ref[i] + timestep_length * (er_ref[i] + scale * r[k])
            outp_ref[i] = vp_ref[i] + timestep_length * (ep_ref[i] + scale * p[k])
        return 0

    lax.fori_loop(0, rows // chunk, synth, 0)


def butterfly(value, axis):
    count = lax.axis_size(axis)
    step = 1
    while step < count:
        value = value + lax.ppermute(value, axis, [(i, i ^ step) for i in range(count)])
        step *= 2
    return value


def neighbours(block, axis):
    count = lax.axis_size(axis)
    up = [(i, i + 1) for i in range(count - 1)]
    low = lax.ppermute(block[:, -1:], axis, up)
    high = lax.ppermute(block[:, :1], axis, [(t, s) for s, t in up])
    return low, high


def on_device(
    surface_mass,
    outward_drift,
    leftover_angular_drift,
    angular_offsets,
    planetesimal_loop_number,
    planetesimal_angle_bin,
    planetesimal_weights,
):
    rows, sector = surface_mass.shape
    blocks = sector // LANES
    whole = blocks * lax.axis_size("az")
    rad_count = lax.axis_size("rad")
    own = lax.axis_index("rad")
    cycle_first = own * rows
    column_first = lax.axis_index("az") * sector
    cell_step = 2.0 * jnp.pi / ANGULAR_BINS
    embryos = planetesimal_weights.shape[0]
    cube = jax.ShapeDtypeStruct((rows, blocks, LANES), f32)

    piled = jnp.stack([surface_mass, outward_drift, leftover_angular_drift])
    gathered = lax.all_gather(piled.reshape(3, rows, blocks, LANES), "az", axis=2, tiled=True)

    columns = column_first + jnp.arange(sector, dtype=jnp.int32).reshape(blocks, LANES)
    cell_angles = (2 * columns + 1).astype(f32) * (jnp.pi / ANGULAR_BINS)
    cos_cell, sin_cell = jnp.cos(cell_angles), jnp.sin(cell_angles)
    embryo_angles = (2 * planetesimal_angle_bin + 1).astype(f32) * (jnp.pi / ANGULAR_BINS)
    embryo_radii = jnp.exp((planetesimal_loop_number.astype(f32) + 0.5) * cell_step)
    emb = jnp.concatenate(
        [
            embryo_radii,
            jnp.cos(embryo_angles),
            jnp.sin(embryo_angles),
            jnp.cos(0.5 * embryo_angles),
            jnp.sin(0.5 * embryo_angles),
        ]
    )
    half_cos, half_sin = jnp.cos(0.5 * cell_angles), jnp.sin(0.5 * cell_angles)
    cycles = cycle_first + jnp.arange(rows, dtype=jnp.int32)
    radius = jnp.exp((cycles.astype(f32) + 0.5) * cell_step)
    area = radius * radius * cell_step * cell_step
    soften = planetesimal_weights ** (-2.0 / 3.0)
    apart = radius[:, None] - embryo_radii[None]
    a_table = (apart * apart + jnp.square(softening * embryo_radii)[None]) * soften[None]
    b_table = 2.0 * radius[:, None] * soften[None]
    a_table, b_table = a_table.reshape(-1), b_table.reshape(-1)

    orders = jnp.arange(MODES, dtype=jnp.int32)

    def turns(phases):
        angles = (phases % (2 * ANGULAR_BINS)).astype(f32) * (jnp.pi / ANGULAR_BINS)
        return jnp.cos(angles), jnp.sin(angles)

    block_first = column_first + LANES * jnp.arange(blocks, dtype=jnp.int32)
    ct, st = turns((2 * block_first + 1)[:, None] * orders[None])
    lanes = jnp.arange(LANES, dtype=jnp.int32)
    table = jnp.concatenate(turns((2 * lanes)[:, None] * orders[None]), axis=1)
    table_t = jnp.concatenate(turns((2 * lanes)[None] * orders[:, None]), axis=0)
    th, tl = split_outside(table)
    tth, ttl = split_outside(table_t)

    radial_emb, azimuthal_emb = call(
        embryo_field,
        (cube, cube),
        [SMEM] * 4 + [VMEM] * 4,
        [pltpu.VMEM((embryos, blocks, LANES), f32)] * 3,
        flops=600_000_000,
    )(a_table, b_table, radius, emb, cos_cell, sin_cell, half_cos, half_sin)

    start = (column_first - angular_offsets) % ANGULAR_BINS
    dens_two, vrad, vphi = call(
        shift_cycles,
        (cube, cube, cube),
        [SMEM, VMEM],
        [pltpu.VMEM((3, whole + blocks + 8, LANES), f32)],
        flops=10_000_000,
    )(start, gathered)

    low, high = neighbours(jnp.stack([dens_two, vrad]), "rad")
    edges = jnp.stack([own == 0, own == rad_count - 1]).astype(jnp.int32)
    transported, partial = call(
        transport,
        (cube, jax.ShapeDtypeStruct((rows, 2 * MODES), f32)),
        [SMEM] + [VMEM] * 8,
        [pltpu.VMEM((8 * blocks, 2 * MODES), f32)],
        flops=400_000_000,
    )(edges, dens_two, vrad, low, high, th, tl, ct, st)
    line = jax.ShapeDtypeStruct((embryos, LANES), f32)
    push_x, push_y = call(
        embryo_push,
        (line, line),
        [SMEM] * 5 + [VMEM] * 5,
        [pltpu.VMEM((rows, blocks, LANES), f32)],
        flops=600_000_000,
    )(a_table, b_table, radius, area, emb, transported, cos_cell, sin_cell, half_cos, half_sin)
    spectra = butterfly(partial * cell_step, "az")
    push = jnp.stack([jnp.sum(push_x, 1), jnp.sum(push_y, 1)]) / planetesimal_weights[None]
    push = butterfly(butterfly(push, "az"), "rad")

    decays = (jnp.arange(MODES, dtype=f32) + 0.5) * cell_step
    decays = jnp.concatenate([decays, decays])
    local = jnp.arange(rows, dtype=f32)
    rise = jnp.exp(-decays[None] * (rows - 1 - local)[:, None])
    fall = jnp.exp(-decays[None] * local[:, None])
    moments = jnp.stack([jnp.sum(rise * spectra, 0), jnp.sum(fall * spectra, 0)])[None]
    every = lax.all_gather(moments, "rad", axis=0, tiled=True)
    others = jnp.arange(rad_count, dtype=jnp.int32)
    gaps = jnp.stack([own - 1 - others, others - own - 1], axis=1)
    weight = jnp.where(
        gaps[:, :, None] >= 0,
        jnp.exp(-(decays * rows) * jnp.maximum(gaps, 0).astype(f32)[:, :, None]),
        0.0,
    )
    carried = jnp.sum(weight * every, 0)
    doubled = jnp.where(orders > 0, 2.0, 1.0).astype(f32)
    radial_weight = jnp.concatenate([doubled, doubled]) * decays * (-1.0 / cell_step)
    azim_weight = jnp.concatenate([doubled * orders, -doubled * orders])
    rates = jnp.stack([decays, jnp.exp(-decays), radial_weight, azim_weight])
    long = rows * blocks
    kicked_r, kicked_p = call(
        kick,
        (cube, cube),
        [SMEM] + [VMEM] * 11,
        [pltpu.VMEM((rows, 2 * MODES), f32)] * 2 + [pltpu.VMEM((long, 2 * MODES), bf16)] * 4,
        flops=400_000_000,
    )(
        radius, spectra, carried, rates, ct, st, tth, ttl, vrad, vphi, radial_emb, azimuthal_emb
    )
    return (
        transported.reshape(rows, sector),
        kicked_r.reshape(rows, sector),
        kicked_p.reshape(rows, sector),
        push,
    )


def solution(mesh):
    placed = (P("rad", "az"), P("rad", "az"), P("rad", "az"), P("rad"), P(), P(), P())
    return jax.shard_map(
        on_device,
        mesh=mesh,
        in_specs=placed,
        out_specs=(P("rad", "az"), P("rad", "az"), P("rad", "az"), P()),
        check_vma=False,
    )
```

time: 333 us -> 204 us (0.61); the launches traced: 328 us -> 203 us
  other arithmetic: 101 us -> 4.28 us
  blocking collectives: 52.2 us -> 8.17 us
  waiting for transfers between devices: 84.8 us -> 127 us
  matrix products: 40.3 us -> 0 us
  Pallas kernels: 0 us -> 32.2 us
  local copies, waits for them, and re-layouts: 27.7 us -> 6.16 us
  starting transfers between devices: 6.74 us -> 11 us
    psum x1 -> x0, blocking collectives: 42.3 us -> none  [on_device(): embryo_disk_acceleration = lax.psum(partial_push, ('rad', 'az'))]
    select_n x16 -> x2, other arithmetic: 40.7 us -> 0.01 us  [the longest x1 0.01 us: on_device(): start = (column_first - angular_offsets) % ANGULAR_BINS]
    dot_general x5 -> x0, matrix products: 40.3 us -> none  [the longest x1 9.47 us: on_device(): jnp.dot(radial_coef, tables, precision=highest)]
    all_gather x1, waiting for transfers between devices: 79.9 us -> 116 us  [on_device(): lax.all_gather(piled.reshape(3, rows, blocks, LANES), 'az', axis=2, tiled...]
    pallas_call x0 -> x5, Pallas kernels: none -> 32.2 us  [the longest x1 10.2 us: on_device(): call(embryo_push, (line, line), [SMEM] * 5 + [VMEM] * 5, [pltpu.VMEM((row...]
    reduce_sum x5 -> x4, other arithmetic: 24.4 us -> 0.43 us  [the longest x1 0.11 us: on_device(): jnp.sum(push_x, 1)]
    slice x28 -> x0, local copies, waits for them, and re-layouts: 21.3 us -> none  [the longest x20 20 us: rotate_cycles(): block = jnp.where(chosen, jnp.roll(block, 2 ** bit_place, axis=2), block)]
    cos x1 -> x2, other arithmetic: 17.9 us -> 1.12 us  [turns(): return (jnp.cos(angles), jnp.sin(angles))]
  transfers between devices with their start and end apart: 6 -> 10, of which waited for: 3 -> 6; matrix products, arithmetic and copies ran while one was open for 16% -> 2% of each run, Pallas kernels for 0% -> 4%
where the time goes in v1:
time: 204 us; the launch traced here: 203 us
  waiting for transfers between devices  127 us (62%)
  Pallas kernels  32.2 us (16%)
  between operations  14.3 us (7%)
  starting transfers between devices  11 us (5%)
  blocking collectives  8.17 us (4%)
  local copies, waits for them, and re-layouts  6.16 us (3%)
  other arithmetic  4.28 us (2%)
    all_gather x1, waiting for transfers between devices, on_device(): lax.all_gather(piled.reshape(3, rows, blocks, LANES), 'az', axis=2, tiled...  116 us
    pallas_call x1, Pallas kernels, on_device(): call(embryo_push, (line, line), [SMEM] * 5 + [VMEM] * 5, [pltpu.VMEM((row...  10.2 us
    ppermute x7, waiting for transfers between devices, butterfly(): lax.ppermute(value, axis, [(i, i ^ step) for i in range(count)])  8.58 us
    all_gather x1, blocking collectives, on_device(): every = lax.all_gather(moments, 'rad', axis=0, tiled=True)  8.17 us
    pallas_call x1, Pallas kernels, on_device(): call(embryo_field, (cube, cube), [SMEM] * 4 + [VMEM] * 4, [pltpu.VMEM((em...  8.08 us
    ppermute x7, starting transfers between devices, butterfly(): lax.ppermute(value, axis, [(i, i ^ step) for i in range(count)])  7.75 us
    pallas_call x1, Pallas kernels, on_device(): call(shift_cycles, (cube, cube, cube), [SMEM, VMEM], [pltpu.VMEM((3, whol...  7.43 us
    unnamed x16, local copies, waits for them, and re-layouts  5.74 us
  transfers between devices with their start and end apart: 10, of which 6 were waited for; matrix products, arithmetic and copies ran while one was open for 2% of the time, Pallas kernels for 4%

profile of v1, /device:TPU:0, one launch (start us, length us, event | category | flops | bytes accessed | tf_op | source)
XLA Modules:
  0.0 203.5 jit_solution(2975983509600119552)
XLA Ops:
  7.2 1.2 copy.13
  8.4 1.1 copy.14
  9.7 1.3 pad_maximum_fusion
  11.3 0.6 fusion.17
  12.0 0.5 fusion.15
  12.8 0.2 fusion.28
  13.0 116.2 %all-gather.4.cloned.1.call-done.g_ref = f32[3,32,128,128]{3,2,1,0:T(8,128)} async-done(((f32[3,32,32,128]{3,2,1,0:T(8,128)}), f32[3,32,128,128]{3,2,1,0:T(8,128)}) %all-gather.4.cloned.1.call-update) | async-done | bytes 6291472 | tf_op jit(solution)/shard_map/all_gather | solution.py:285
  129.2 7.4 %shard_map.102 = (f32[32,32,128]{2,1,0:T(8,128)S(1)}, f32[32,32,128]{2,1,0:T(8,128)S(1)}, f32[32,32,128]{2,1,0:T(8,128)S(1)}) custom-call(s32[32]{0:T(128)S(1)} %and_select_fusion.start_ref, f32[3,32,128,128]{3,2,1,0:T(8,128)} %all-gather.4.cloned.1.call-done.g_ref), custom_call_target="tpu_custom_call" | custom-call | flops 10000000 | bytes 1048576 | tf_op jit(solution)/shard_map/pallas_call | solution.py:334
  136.6 1.9 collective-permute-start
  138.5 1.3 collective-permute-start.1
  140.1 2.6 %collective-permute-done.1.high_ref = f32[2,1,32,128]{3,2,1,0:T(8,128)S(1)} collective-permute-done((f32[2,1,32,128]{3,2,1,0:T(8,128)S(1)}, f32[2,1,32,128]{3,2,1,0:T(8,128)S(1)}, u32[]{:S(2)}, u32[]{:S(2)}) %collective-permute-start.1) | collective-permute-done | bytes 32800 | tf_op jit(solution)/shard_map/ppermute | solution.py:260
  142.7 2.3 %shard_map.103 = (f32[32,32,128]{2,1,0:T(8,128)S(1)}, f32[32,512]{1,0:T(8,128)S(1)}) custom-call(s32[2]{0:T(128)S(1)} %add_convert_fusion.edge_ref, f32[32,32,128]{2,1,0:T(8,128)S(1)} %get-tuple-element.15.d_ref, f32[32,32,128]{2,1,0:T(8,128)S(1)} %get-tuple-element.16.v_ref.vr_ref, f32[2,1,32,128]{3,2,1,0:T(8,128)S(1)} %collective-permute-done.low_ref, ...), custom_call_target="tpu_custom_call" | custom-call | flops 400000000 | bytes 1048576 | tf_op jit(solution)/shard_map/pallas_call | solution.py:344
  145.0 10.2 %shard_map.106 = (f32[32,128]{1,0:T(8,128)S(1)}, f32[32,128]{1,0:T(8,128)S(1)}) custom-call(f32[1024]{0:T(1024)S(1)} %mul.389.a_ref, f32[1024]{0:T(1024)S(1)} %mul.394.b_ref, f32[32]{0:T(128)S(1)} %multiply_exponential_fusion.1.r_ref, f32[32]{0:T(128)S(1)} %multiply_multiply_fusion.area_ref, f32[160]{0:T(256)S(1)} %concatenate.73.emb_ref, ...), custom_call_target="tpu_custom_call" | custom-call | flops 600000000 | bytes 1048576 | tf_op jit(solution)/shard_map/pallas_call | solution.py:352
  155.2 0.1 reduce_sum.48
  155.4 0.1 reduce_sum.49
  155.6 3.5 %collective-permute-done.4 = f32[2,32]{1,0:T(2,128)S(1)} collective-permute-done((f32[2,32]{1,0:T(2,128)S(1)}, f32[2,32]{1,0:T(2,128)S(1)}, u32[]{:S(2)}, u32[]{:S(2)}) %collective-permute-start.4) | collective-permute-done | bytes 288 | tf_op jit(solution)/shard_map/ppermute | solution.py:251
  159.1 0.7 collective-permute-start.5
  159.8 0.5 collective-permute-start.2
  160.3 3.4 %collective-permute-done.5 = f32[2,32]{1,0:T(2,128)S(1)} collective-permute-done((f32[2,32]{1,0:T(2,128)S(1)}, f32[2,32]{1,0:T(2,128)S(1)}, u32[]{:S(2)}, u32[]{:S(2)}) %collective-permute-start.5) | collective-permute-done | bytes 288 | tf_op jit(solution)/shard_map/ppermute | solution.py:251
  163.7 0.4 collective-permute-start.6
  164.1 0.8 collective-permute-done.6
  164.9 2.5 %collective-permute-start.7 = (f32[2,32]{1,0:T(2,128)S(1)}, f32[2,32]{1,0:T(2,128)S(1)}, u32[]{:S(2)}, u32[]{:S(2)}) collective-permute-start(f32[2,32]{1,0:T(2,128)S(1)} %add.181), channel_id=1, source_target_pairs={{0,8},{4,12},{8,0},{12,4},{16,24},{20,28},{24,16},{28,20},{1,9},{5... | collective-permute-start | bytes 776 | tf_op jit(solution)/shard_map/ppermute | solution.py:251
  167.5 0.7 collective-permute-start.3
  168.1 0.9 collective-permute-done.7
  169.0 2.9 %collective-permute-start.8 = (f32[2,32]{1,0:T(2,128)S(1)}, f32[2,32]{1,0:T(2,128)S(1)}, u32[]{:S(2)}, u32[]{:S(2)}) collective-permute-start(f32[2,32]{1,0:T(2,128)S(1)} %add.182), channel_id=1, source_target_pairs={{0,16},{4,20},{8,24},{12,28},{16,0},{20,4},{24,8},{28,12},{1,17},{... | collective-permute-start | bytes 776 | tf_op jit(solution)/shard_map/ppermute | solution.py:251
  171.9 8.1 %shard_map.104 = (f32[32,32,128]{2,1,0:T(8,128)S(1)}, f32[32,32,128]{2,1,0:T(8,128)S(1)}) custom-call(f32[1024]{0:T(1024)S(1)} %mul.389.a_ref, f32[1024]{0:T(1024)S(1)} %mul.394.b_ref, f32[32]{0:T(128)S(1)} %multiply_exponential_fusion.1.r_ref, f32[160]{0:T(256)S(1)} %concatenate.73.emb_ref, f32[32,128]{1,0:T(8,128)S(1)} %get-tuple-element.55.cos_ref, ...), custom_call_target="tpu_custom_call" | custom-call | flops 600000000 | bytes 1048576 | tf_op jit(solution)/shard_map/pallas_call | solution.py:325
  180.2 1.1 copy.24
  181.3 0.6 add.183
  182.0 8.2 %all-gather.1 = f32[8,2,512]{2,1,0:T(2,128)S(1)} all-gather(f32[1,2,512]{2,1,0:T(2,128)S(1)} %maximum_bitcast_fusion), channel_id=2, replica_groups=mesh['rad'=8,'az'=4] {'rad'}, dimensions={0}, use_global_device_ids=true | all-gather | bytes 36864 | tf_op jit(solution)/shard_map/all_gather | solution.py:369
  190.3 4.2 %shard_map.105 = (f32[32,32,128]{2,1,0:T(8,128)S(1)}, f32[32,32,128]{2,1,0:T(8,128)S(1)}) custom-call(f32[32]{0:T(128)S(1)} %multiply_exponential_fusion.1.r_ref, f32[32,512]{1,0:T(8,128)S(1)} %get-tuple-element.28.x_ref, f32[2,512]{1,0:T(2,128)S(1)} %multiply_reduce_fusion.2.from_ref, f32[4,512]{1,0:T(4,128)S(1)} %pad_maximum_fusion.5.rate_ref, ...), custom_call_target="tpu_custom_call" | custom-call | flops 400000000 | bytes 1048576 | tf_op jit(solution)/shard_map/pallas_call | solution.py:383
  194.4 1.1 copy.22
  195.5 1.1 copy.23
  (59 shorter events, 1.6 us)
Async XLA Ops:
  7.2 2.4 %copy-start = (f32[32,4096]{1,0:T(8,128)S(1)}, f32[32,4096]{1,0:T(8,128)}, u32[]{:S(2)}) copy-start(f32[32,4096]{1,0:T(8,128)} %param.9) | copy-start | bytes 1572868
  7.2 122.0 %all-gather.4.cloned.1.call-start = ((), (), s32[]{:S(2)}) async-start(), calls=%async_computation | async-start | bytes 7864320 | tf_op jit(solution)/shard_map/all_gather | solution.py:285
  10.9 1.6 copy-start.4
  10.9 1.7 copy-start.1
  10.9 1.7 copy-start.2
  10.9 1.7 copy-start.3
  136.6 3.5 %collective-permute-start = (f32[2,1,32,128]{3,2,1,0:T(8,128)S(1)}, f32[2,1,32,128]{3,2,1,0:T(8,128)S(1)}, u32[]{:S(2)}, u32[]{:S(2)}) collective-permute-start(f32[2,1,32,128]{3,2,1,0:T(8,128)S(1)} %get-tuple-element.30), channel_id=1, source_target_pairs={{0,4},{4,8},{8,12},{12,16},{16,20},{20,24},{24,28},{1,5},{5,9},{9,... | collective-permute-start | bytes 98312 | tf_op jit(solution)/shard_map/ppermute | solution.py:259
  138.5 4.2 %collective-permute-start.1 = (f32[2,1,32,128]{3,2,1,0:T(8,128)S(1)}, f32[2,1,32,128]{3,2,1,0:T(8,128)S(1)}, u32[]{:S(2)}, u32[]{:S(2)}) collective-permute-start(f32[2,1,32,128]{3,2,1,0:T(8,128)S(1)} %get-tuple-element.29), channel_id=1, source_target_pairs={{4,0},{8,4},{12,8},{16,12},{20,16},{24,20},{28,24},{5,1},{9,5},{13... | collective-permute-start | bytes 98312 | tf_op jit(solution)/shard_map/ppermute | solution.py:260
  155.5 3.6 %collective-permute-start.4 = (f32[2,32]{1,0:T(2,128)S(1)}, f32[2,32]{1,0:T(2,128)S(1)}, u32[]{:S(2)}, u32[]{:S(2)}) collective-permute-start(f32[2,32]{1,0:T(2,128)S(1)} %maximum_divide_fusion), channel_id=1, source_target_pairs={{0,1},{1,0},{2,3},{3,2},{4,5},{5,4},{6,7},{7,6},{8,9},{9,8},{10,11... | collective-permute-start | bytes 776 | tf_op jit(solution)/shard_map/ppermute | solution.py:251
  159.1 4.5 %collective-permute-start.5 = (f32[2,32]{1,0:T(2,128)S(1)}, f32[2,32]{1,0:T(2,128)S(1)}, u32[]{:S(2)}, u32[]{:S(2)}) collective-permute-start(f32[2,32]{1,0:T(2,128)S(1)} %fusion.38), channel_id=1, source_target_pairs={{0,2},{1,3},{2,0},{3,1},{4,6},{5,7},{6,4},{7,5},{8,10},{9,11},{10,... | collective-permute-start | bytes 776 | tf_op jit(solution)/shard_map/ppermute | solution.py:251
  159.8 7.6 %collective-permute-start.2 = (f32[32,512]{1,0:T(8,128)S(1)}, f32[32,512]{1,0:T(8,128)S(1)}, u32[]{:S(2)}, u32[]{:S(2)}) collective-permute-start(f32[32,512]{1,0:T(8,128)S(1)} %broadcast_multiply_fusion), channel_id=1, source_target_pairs={{0,1},{1,0},{2,3},{3,2},{4,5},{5,4},{6,7},{7,6},{8,9},{9,8},{10,11... | collective-permute-start | bytes 196616 | tf_op jit(solution)/shard_map/ppermute | solution.py:251
  163.7 1.2 collective-permute-start.6
  164.9 4.1 %collective-permute-start.7 = (f32[2,32]{1,0:T(2,128)S(1)}, f32[2,32]{1,0:T(2,128)S(1)}, u32[]{:S(2)}, u32[]{:S(2)}) collective-permute-start(f32[2,32]{1,0:T(2,128)S(1)} %add.181), channel_id=1, source_target_pairs={{0,8},{4,12},{8,0},{12,4},{16,24},{20,28},{24,16},{28,20},{1,9},{5... | collective-permute-start | bytes 776 | tf_op jit(solution)/shard_map/ppermute | solution.py:251
  167.5 14.4 %collective-permute-start.3 = (f32[32,512]{1,0:T(8,128)S(1)}, f32[32,512]{1,0:T(8,128)S(1)}, u32[]{:S(2)}, u32[]{:S(2)}) collective-permute-start(f32[32,512]{1,0:T(8,128)S(1)} %fusion.37), channel_id=1, source_target_pairs={{0,2},{1,3},{2,0},{3,1},{4,6},{5,7},{6,4},{7,5},{8,10},{9,11},{10,... | collective-permute-start | bytes 196616 | tf_op jit(solution)/shard_map/ppermute | solution.py:251
  169.0 12.3 %collective-permute-start.8 = (f32[2,32]{1,0:T(2,128)S(1)}, f32[2,32]{1,0:T(2,128)S(1)}, u32[]{:S(2)}, u32[]{:S(2)}) collective-permute-start(f32[2,32]{1,0:T(2,128)S(1)} %add.182), channel_id=1, source_target_pairs={{0,16},{4,20},{8,24},{12,28},{16,0},{20,4},{24,8},{28,12},{1,17},{... | collective-permute-start | bytes 776 | tf_op jit(solution)/shard_map/ppermute | solution.py:251
Sparse Core Ops, SparseCore 0:
  11.1 118.0 all-gather.3

commit v2 on v1

--- a/solution.py
+++ b/solution.py
@@ -68,9 +68,77 @@
     lax.fori_loop(0, rad_ref.shape[0], row, 0)
 
 
+def ring_gather(own_ref, out_ref, keep_sem, send_sem, recv_sem):
+    me = lax.axis_index("az")
+    right, left = (me + 1) % 4, (me + 3) % 4
+    half = own_ref.shape[1] // 2
+    barrier = pltpu.get_barrier_semaphore()
+    for peer in (left, right):
+        pl.semaphore_signal(
+            barrier, inc=1, device_id={"az": peer}, device_id_type=pl.DeviceIdType.MESH
+        )
+    pl.semaphore_wait(barrier, 2)
+
+    def copy(k, source, slot, part, peer):
+        rows = pl.ds(part * half, half)
+        return pltpu.make_async_remote_copy(
+            src_ref=source.at[:, rows],
+            dst_ref=out_ref.at[slot, :, rows],
+            send_sem=send_sem.at[k],
+            recv_sem=recv_sem.at[k],
+            device_id={"az": peer},
+            device_id_type=pl.DeviceIdType.MESH,
+        )
+
+    firsts = [
+        copy(0, own_ref, me, 0, right),
+        copy(1, own_ref, me, 1, left),
+        copy(2, own_ref, me, 1, right),
+        copy(3, own_ref, me, 0, left),
+    ]
+    for c in firsts:
+        c.start()
+    keep = pltpu.make_async_copy(own_ref, out_ref.at[me], keep_sem)
+    keep.start()
+    firsts[0].wait_recv()
+    onward = copy(4, out_ref.at[left], left, 0, right)
+    onward.start()
+    firsts[1].wait_recv()
+    back = copy(5, out_ref.at[right], right, 1, left)
+    back.start()
+    firsts[2].wait_recv()
+    firsts[3].wait_recv()
+    onward.wait_recv()
+    back.wait_recv()
+    for c in firsts + [onward, back]:
+        c.wait_send()
+    keep.wait()
+
+
+def gather_sectors(piled):
+    count = lax.axis_size("az")
+    if count != 4:
+        return lax.all_gather(piled, "az", axis=0)
+    return pl.pallas_call(
+        ring_gather,
+        out_shape=jax.ShapeDtypeStruct((count,) + piled.shape, f32),
+        in_specs=[VMEM],
+        out_specs=VMEM,
+        scratch_shapes=[
+            pltpu.SemaphoreType.DMA,
+            pltpu.SemaphoreType.DMA((6,)),
+            pltpu.SemaphoreType.DMA((6,)),
+        ],
+        compiler_params=pltpu.CompilerParams(
+            collective_id=0, has_side_effects=True, vmem_limit_bytes=48 * 1024 * 1024
+        ),
+    )(piled)
+
+
 def shift_cycles(start_ref, g_ref, dens_ref, vrad_ref, vphi_ref, line_ref):
     rows, blocks = dens_ref.shape[:2]
-    whole = g_ref.shape[2]
+    sectors = g_ref.shape[0]
+    whole = sectors * blocks
     total = whole * LANES
     extra = line_ref.shape[1] - whole
     lane = lax.broadcasted_iota(jnp.int32, (blocks, LANES), 1)
@@ -84,8 +152,10 @@
 
     def row(i, _):
         for field in range(3):
-            line_ref[field, :whole] = g_ref[field, i]
-            line_ref[field, whole:] = g_ref[field, i, :extra]
+            for k in range(sectors):
+                line_ref[field, k * blocks : (k + 1) * blocks] = g_ref[k, field, i]
+            line_ref[field, whole : whole + blocks] = g_ref[0, field, i]
+            line_ref[field, whole + blocks :] = g_ref[1 % sectors, field, i, : extra - blocks]
         here = start_ref[i]
         below = (here + total - 1) % total
         above = (here + 1) % total
@@ -282,7 +352,7 @@
     cube = jax.ShapeDtypeStruct((rows, blocks, LANES), f32)
 
     piled = jnp.stack([surface_mass, outward_drift, leftover_angular_drift])
-    gathered = lax.all_gather(piled.reshape(3, rows, blocks, LANES), "az", axis=2, tiled=True)
+    gathered = gather_sectors(piled.reshape(3, rows, blocks, LANES))
 
     columns = column_first + jnp.arange(sector, dtype=jnp.int32).reshape(blocks, LANES)
     cell_angles = (2 * columns + 1).astype(f32) * (jnp.pi / ANGULAR_BINS)

time: 204 us -> 182 us (0.89)
  waiting for transfers between devices: 127 us -> 4.24 us
  Pallas kernels: 32.2 us -> 141 us
  between operations: 14.3 us -> 0.99 us
  starting transfers between devices: 11 us -> 17.1 us
    all_gather x1 -> x0, waiting for transfers between devices: 116 us -> none  [on_device(): lax.all_gather(piled.reshape(3, rows, blocks, LANES), 'az', axis=2, tiled...]
    pallas_call x0 -> x1, Pallas kernels: none -> 109 us  [gather_sectors(): pl.pallas_call(ring_gather, out_shape=jax.ShapeDtypeStruct((count,) + pil...]
    ppermute x7, starting transfers between devices: 7.75 us -> 14.5 us  [butterfly(): lax.ppermute(value, axis, [(i, i ^ step) for i in range(count)])]
    ppermute x7, waiting for transfers between devices: 8.58 us -> 3 us  [butterfly(): lax.ppermute(value, axis, [(i, i ^ step) for i in range(count)])]
  transfers between devices with their start and end apart: 10 -> 9, of which waited for: 6 -> 3; matrix products, arithmetic and copies ran while one was open for 2% -> 2% of each run, Pallas kernels for 4% -> 4%
where the time goes in v2:
time: 182 us
  Pallas kernels  141 us (77%)
  starting transfers between devices  17.1 us (9%)
  blocking collectives  8.62 us (5%)
  local copies, waits for them, and re-layouts  6.18 us (3%)
  waiting for transfers between devices  4.24 us (2%)
  other arithmetic  3.12 us (2%)
    pallas_call x1, Pallas kernels, gather_sectors(): pl.pallas_call(ring_gather, out_shape=jax.ShapeDtypeStruct((count,) + pil...  109 us
    ppermute x7, starting transfers between devices, butterfly(): lax.ppermute(value, axis, [(i, i ^ step) for i in range(count)])  14.5 us
    pallas_call x1, Pallas kernels, on_device(): call(embryo_push, (line, line), [SMEM] * 5 + [VMEM] * 5, [pltpu.VMEM((row...  10.2 us
    all_gather x1, blocking collectives, on_device(): every = lax.all_gather(moments, 'rad', axis=0, tiled=True)  8.62 us
    pallas_call x1, Pallas kernels, on_device(): call(embryo_field, (cube, cube), [SMEM] * 4 + [VMEM] * 4, [pltpu.VMEM((em...  8.08 us
    pallas_call x1, Pallas kernels, on_device(): call(shift_cycles, (cube, cube, cube), [SMEM, VMEM], [pltpu.VMEM((3, whol...  7.43 us
    unnamed x16, local copies, waits for them, and re-layouts  5.76 us
    pallas_call x1, Pallas kernels, on_device(): call(kick, (cube, cube), [SMEM] + [VMEM] * 11, [pltpu.VMEM((rows, 2 * MOD...  4.17 us
  transfers between devices with their start and end apart: 9, of which 3 were waited for; matrix products, arithmetic and copies ran while one was open for 2% of the time, Pallas kernels for 4%

profile of v2, /device:TPU:0, one launch (start us, length us, event | category | flops | bytes accessed | tf_op | source)
XLA Modules:
  0.0 181.5 jit_solution(18062473711997098655)
XLA Ops:
  0.6 1.2 copy.13
  1.8 1.1 copy.14
  3.1 0.1 pad_maximum_fusion.own_ref
  3.2 109.1 %shard_map.102.g_ref = f32[4,3,32,32,128]{4,3,2,1,0:T(8,128)} custom-call(f32[3,32,32,128]{3,2,1,0:T(8,128)S(1)} %pad_maximum_fusion.own_ref), custom_call_target="tpu_custom_call" | custom-call | tf_op jit(solution)/shard_map/pallas_call | solution.py:122
  112.3 7.4 %shard_map.103 = (f32[32,32,128]{2,1,0:T(8,128)S(1)}, f32[32,32,128]{2,1,0:T(8,128)S(1)}, f32[32,32,128]{2,1,0:T(8,128)S(1)}) custom-call(s32[32]{0:T(128)S(1)} %get-tuple-element.58.start_ref, f32[4,3,32,32,128]{4,3,2,1,0:T(8,128)} %shard_map.102.g_ref), custom_call_target="tpu_custom_call" | custom-call | flops 10000000 | bytes 1048576 | tf_op jit(solution)/shard_map/pallas_call | solution.py:404
  119.8 1.3 collective-permute-start
  121.1 1.3 collective-permute-start.1
  122.7 0.6 fusion.17
  123.3 0.5 fusion.15
  123.8 0.2 fusion.28
  124.7 1.2 collective-permute-done.1.high_ref
  125.9 2.3 %shard_map.104 = (f32[32,32,128]{2,1,0:T(8,128)S(1)}, f32[32,512]{1,0:T(8,128)S(1)}) custom-call(s32[2]{0:T(128)S(1)} %add_convert_fusion.edge_ref, f32[32,32,128]{2,1,0:T(8,128)S(1)} %get-tuple-element.15.d_ref, f32[32,32,128]{2,1,0:T(8,128)S(1)} %get-tuple-element.16.v_ref.vr_ref, f32[2,1,32,128]{3,2,1,0:T(8,128)S(1)} %collective-permute-done.low_ref, ...), custom_call_target="tpu_custom_call" | custom-call | flops 400000000 | bytes 1048576 | tf_op jit(solution)/shard_map/pallas_call | solution.py:414
  128.3 10.2 %shard_map.107 = (f32[32,128]{1,0:T(8,128)S(1)}, f32[32,128]{1,0:T(8,128)S(1)}) custom-call(f32[1024]{0:T(1024)S(1)} %mul.389.a_ref, f32[1024]{0:T(1024)S(1)} %mul.394.b_ref, f32[32]{0:T(128)S(1)} %multiply_exponential_fusion.1.r_ref, f32[32]{0:T(128)S(1)} %multiply_multiply_fusion.area_ref, f32[160]{0:T(256)S(1)} %concatenate.73.emb_ref, ...), custom_call_target="tpu_custom_call" | custom-call | flops 600000000 | bytes 1048576 | tf_op jit(solution)/shard_map/pallas_call | solution.py:422
  138.5 0.1 reduce_sum.48
  138.6 0.1 reduce_sum.49
  138.7 1.4 collective-permute-start.4
  140.2 2.2 %collective-permute-done.4 = f32[2,32]{1,0:T(2,128)S(1)} collective-permute-done((f32[2,32]{1,0:T(2,128)S(1)}, f32[2,32]{1,0:T(2,128)S(1)}, u32[]{:S(2)}, u32[]{:S(2)}) %collective-permute-start.4) | collective-permute-done | bytes 288 | tf_op jit(solution)/shard_map/ppermute | solution.py:321
  142.4 2.9 %collective-permute-start.5 = (f32[2,32]{1,0:T(2,128)S(1)}, f32[2,32]{1,0:T(2,128)S(1)}, u32[]{:S(2)}, u32[]{:S(2)}) collective-permute-start(f32[2,32]{1,0:T(2,128)S(1)} %fusion.38), channel_id=1, source_target_pairs={{0,2},{1,3},{2,0},{3,1},{4,6},{5,7},{6,4},{7,5},{8,10},{9,11},{10,... | collective-permute-start | bytes 776 | tf_op jit(solution)/shard_map/ppermute | solution.py:321
  145.3 2.1 %collective-permute-start.2 = (f32[32,512]{1,0:T(8,128)S(1)}, f32[32,512]{1,0:T(8,128)S(1)}, u32[]{:S(2)}, u32[]{:S(2)}) collective-permute-start(f32[32,512]{1,0:T(8,128)S(1)} %broadcast_multiply_fusion), channel_id=1, source_target_pairs={{0,1},{1,0},{2,3},{3,2},{4,5},{5,4},{6,7},{7,6},{8,9},{9,8},{10,11... | collective-permute-start | bytes 196616 | tf_op jit(solution)/shard_map/ppermute | solution.py:321
  147.4 1.0 collective-permute-start.6
  148.4 0.8 collective-permute-done.6
  149.2 2.7 %collective-permute-start.7 = (f32[2,32]{1,0:T(2,128)S(1)}, f32[2,32]{1,0:T(2,128)S(1)}, u32[]{:S(2)}, u32[]{:S(2)}) collective-permute-start(f32[2,32]{1,0:T(2,128)S(1)} %add.181), channel_id=1, source_target_pairs={{0,8},{4,12},{8,0},{12,4},{16,24},{20,28},{24,16},{28,20},{1,9},{5... | collective-permute-start | bytes 776 | tf_op jit(solution)/shard_map/ppermute | solution.py:321
  151.9 2.4 %collective-permute-start.3 = (f32[32,512]{1,0:T(8,128)S(1)}, f32[32,512]{1,0:T(8,128)S(1)}, u32[]{:S(2)}, u32[]{:S(2)}) collective-permute-start(f32[32,512]{1,0:T(8,128)S(1)} %fusion.37), channel_id=1, source_target_pairs={{0,2},{1,3},{2,0},{3,1},{4,6},{5,7},{6,4},{7,5},{8,10},{9,11},{10,... | collective-permute-start | bytes 196616 | tf_op jit(solution)/shard_map/ppermute | solution.py:321
  154.3 2.0 %collective-permute-start.8 = (f32[2,32]{1,0:T(2,128)S(1)}, f32[2,32]{1,0:T(2,128)S(1)}, u32[]{:S(2)}, u32[]{:S(2)}) collective-permute-start(f32[2,32]{1,0:T(2,128)S(1)} %add.182), channel_id=1, source_target_pairs={{0,16},{4,20},{8,24},{12,28},{16,0},{20,4},{24,8},{28,12},{1,17},{... | collective-permute-start | bytes 776 | tf_op jit(solution)/shard_map/ppermute | solution.py:321
  156.3 8.1 %shard_map.105 = (f32[32,32,128]{2,1,0:T(8,128)S(1)}, f32[32,32,128]{2,1,0:T(8,128)S(1)}) custom-call(f32[1024]{0:T(1024)S(1)} %mul.389.a_ref, f32[1024]{0:T(1024)S(1)} %mul.394.b_ref, f32[32]{0:T(128)S(1)} %multiply_exponential_fusion.1.r_ref, f32[160]{0:T(256)S(1)} %concatenate.73.emb_ref, f32[32,128]{1,0:T(8,128)S(1)} %get-tuple-element.55.cos_ref, ...), custom_call_target="tpu_custom_call" | custom-call | flops 600000000 | bytes 1048576 | tf_op jit(solution)/shard_map/pallas_call | solution.py:395
  164.6 1.1 copy.24
  165.7 0.6 add.183
  166.4 8.6 %all-gather.1 = f32[8,2,512]{2,1,0:T(2,128)S(1)} all-gather(f32[1,2,512]{2,1,0:T(2,128)S(1)} %maximum_bitcast_fusion), channel_id=2, replica_groups=mesh['rad'=8,'az'=4] {'rad'}, dimensions={0}, use_global_device_ids=true | all-gather | bytes 36864 | tf_op jit(solution)/shard_map/all_gather | solution.py:439
  175.0 0.1 multiply_reduce_fusion.2.from_ref
  175.1 4.2 %shard_map.106 = (f32[32,32,128]{2,1,0:T(8,128)S(1)}, f32[32,32,128]{2,1,0:T(8,128)S(1)}) custom-call(f32[32]{0:T(128)S(1)} %multiply_exponential_fusion.1.r_ref, f32[32,512]{1,0:T(8,128)S(1)} %get-tuple-element.28.x_ref, f32[2,512]{1,0:T(2,128)S(1)} %multiply_reduce_fusion.2.from_ref, f32[4,512]{1,0:T(4,128)S(1)} %pad_maximum_fusion.5.rate_ref, ...), custom_call_target="tpu_custom_call" | custom-call | flops 400000000 | bytes 1048576 | tf_op jit(solution)/shard_map/pallas_call | solution.py:453
  179.3 1.1 copy.22
  180.4 1.1 copy.23
  (56 shorter events, 1.3 us)
Async XLA Ops:
  0.6 2.4 %copy-start = (f32[32,4096]{1,0:T(8,128)S(1)}, f32[32,4096]{1,0:T(8,128)}, u32[]{:S(2)}) copy-start(f32[32,4096]{1,0:T(8,128)} %param.9) | copy-start | bytes 1572868
  3.2 109.1 %copy-start.4 = (s32[32]{0:T(128)S(1)}, s32[32]{0:T(128)}, u32[]{:S(2)}) copy-start(s32[32]{0:T(128)} %param.10) | copy-start | bytes 388
  119.8 4.3 %copy-start.2 = (s32[32]{0:T(128)S(1)}, s32[32]{0:T(128)}, u32[]{:S(2)}) copy-start(s32[32]{0:T(128)} %param.11) | copy-start | bytes 388
  119.8 4.3 %copy-start.1 = (f32[32]{0:T(128)S(1)}, f32[32]{0:T(128)}, u32[]{:S(2)}) copy-start(f32[32]{0:T(128)} %param.13) | copy-start | bytes 388
  119.8 4.3 %copy-start.3 = (s32[32]{0:T(128)S(1)}, s32[32]{0:T(128)}, u32[]{:S(2)}) copy-start(s32[32]{0:T(128)} %param.12) | copy-start | bytes 388
  119.8 4.9 %collective-permute-start = (f32[2,1,32,128]{3,2,1,0:T(8,128)S(1)}, f32[2,1,32,128]{3,2,1,0:T(8,128)S(1)}, u32[]{:S(2)}, u32[]{:S(2)}) collective-permute-start(f32[2,1,32,128]{3,2,1,0:T(8,128)S(1)} %get-tuple-element.30), channel_id=1, source_target_pairs={{0,4},{4,8},{8,12},{12,16},{16,20},{20,24},{24,28},{1,5},{5,9},{9,... | collective-permute-start | bytes 98312 | tf_op jit(solution)/shard_map/ppermute | solution.py:329
  121.1 4.8 %collective-permute-start.1 = (f32[2,1,32,128]{3,2,1,0:T(8,128)S(1)}, f32[2,1,32,128]{3,2,1,0:T(8,128)S(1)}, u32[]{:S(2)}, u32[]{:S(2)}) collective-permute-start(f32[2,1,32,128]{3,2,1,0:T(8,128)S(1)} %get-tuple-element.29), channel_id=1, source_target_pairs={{4,0},{8,4},{12,8},{16,12},{20,16},{24,20},{28,24},{5,1},{9,5},{13... | collective-permute-start | bytes 98312 | tf_op jit(solution)/shard_map/ppermute | solution.py:330
  138.7 3.6 %collective-permute-start.4 = (f32[2,32]{1,0:T(2,128)S(1)}, f32[2,32]{1,0:T(2,128)S(1)}, u32[]{:S(2)}, u32[]{:S(2)}) collective-permute-start(f32[2,32]{1,0:T(2,128)S(1)} %maximum_divide_fusion), channel_id=1, source_target_pairs={{0,1},{1,0},{2,3},{3,2},{4,5},{5,4},{6,7},{7,6},{8,9},{9,8},{10,11... | collective-permute-start | bytes 776 | tf_op jit(solution)/shard_map/ppermute | solution.py:321
  142.4 5.0 %collective-permute-start.5 = (f32[2,32]{1,0:T(2,128)S(1)}, f32[2,32]{1,0:T(2,128)S(1)}, u32[]{:S(2)}, u32[]{:S(2)}) collective-permute-start(f32[2,32]{1,0:T(2,128)S(1)} %fusion.38), channel_id=1, source_target_pairs={{0,2},{1,3},{2,0},{3,1},{4,6},{5,7},{6,4},{7,5},{8,10},{9,11},{10,... | collective-permute-start | bytes 776 | tf_op jit(solution)/shard_map/ppermute | solution.py:321
  145.3 6.6 %collective-permute-start.2 = (f32[32,512]{1,0:T(8,128)S(1)}, f32[32,512]{1,0:T(8,128)S(1)}, u32[]{:S(2)}, u32[]{:S(2)}) collective-permute-start(f32[32,512]{1,0:T(8,128)S(1)} %broadcast_multiply_fusion), channel_id=1, source_target_pairs={{0,1},{1,0},{2,3},{3,2},{4,5},{5,4},{6,7},{7,6},{8,9},{9,8},{10,11... | collective-permute-start | bytes 196616 | tf_op jit(solution)/shard_map/ppermute | solution.py:321
  147.4 1.8 collective-permute-start.6
  149.2 5.2 %collective-permute-start.7 = (f32[2,32]{1,0:T(2,128)S(1)}, f32[2,32]{1,0:T(2,128)S(1)}, u32[]{:S(2)}, u32[]{:S(2)}) collective-permute-start(f32[2,32]{1,0:T(2,128)S(1)} %add.181), channel_id=1, source_target_pairs={{0,8},{4,12},{8,0},{12,4},{16,24},{20,28},{24,16},{28,20},{1,9},{5... | collective-permute-start | bytes 776 | tf_op jit(solution)/shard_map/ppermute | solution.py:321
  151.9 14.4 %collective-permute-start.3 = (f32[32,512]{1,0:T(8,128)S(1)}, f32[32,512]{1,0:T(8,128)S(1)}, u32[]{:S(2)}, u32[]{:S(2)}) collective-permute-start(f32[32,512]{1,0:T(8,128)S(1)} %fusion.37), channel_id=1, source_target_pairs={{0,2},{1,3},{2,0},{3,1},{4,6},{5,7},{6,4},{7,5},{8,10},{9,11},{10,... | collective-permute-start | bytes 196616 | tf_op jit(solution)/shard_map/ppermute | solution.py:321
  154.3 11.4 %collective-permute-start.8 = (f32[2,32]{1,0:T(2,128)S(1)}, f32[2,32]{1,0:T(2,128)S(1)}, u32[]{:S(2)}, u32[]{:S(2)}) collective-permute-start(f32[2,32]{1,0:T(2,128)S(1)} %add.182), channel_id=1, source_target_pairs={{0,16},{4,20},{8,24},{12,28},{16,0},{20,4},{24,8},{28,12},{1,17},{... | collective-permute-start | bytes 776 | tf_op jit(solution)/shard_map/ppermute | solution.py:321

commit v3 on v2

--- a/solution.py
+++ b/solution.py
@@ -68,7 +68,9 @@
     lax.fori_loop(0, rad_ref.shape[0], row, 0)
 
 
-def ring_gather(own_ref, out_ref, keep_sem, send_sem, recv_sem):
+def ring_gather(own_ref, *refs):
+    *field_refs, keep_sem, send_sem, recv_sem = refs
+    out_ref = field_refs.pop(8)
     me = lax.axis_index("az")
     right, left = (me + 1) % 4, (me + 3) % 4
     half = own_ref.shape[1] // 2
@@ -100,6 +102,7 @@
         c.start()
     keep = pltpu.make_async_copy(own_ref, out_ref.at[me], keep_sem)
     keep.start()
+    embryo_field(*field_refs)
     firsts[0].wait_recv()
     onward = copy(4, out_ref.at[left], left, 0, right)
     onward.start()
@@ -115,16 +118,22 @@
     keep.wait()
 
 
-def gather_sectors(piled):
+def gather_sectors(piled, tables, embryos):
     count = lax.axis_size("az")
+    cube = jax.ShapeDtypeStruct(piled.shape[1:], f32)
+    scratch = [pltpu.VMEM((embryos,) + piled.shape[2:], f32)] * 3
     if count != 4:
-        return lax.all_gather(piled, "az", axis=0)
+        fields = call(
+            embryo_field, (cube, cube), [SMEM] * 4 + [VMEM] * 4, scratch, flops=600_000_000
+        )(*tables)
+        return (lax.all_gather(piled, "az", axis=0),) + tuple(fields)
     return pl.pallas_call(
         ring_gather,
-        out_shape=jax.ShapeDtypeStruct((count,) + piled.shape, f32),
-        in_specs=[VMEM],
-        out_specs=VMEM,
+        out_shape=(jax.ShapeDtypeStruct((count,) + piled.shape, f32), cube, cube),
+        in_specs=[VMEM] + [SMEM] * 4 + [VMEM] * 4,
+        out_specs=(VMEM,) * 3,
         scratch_shapes=[
+            *scratch,
             pltpu.SemaphoreType.DMA,
             pltpu.SemaphoreType.DMA((6,)),
             pltpu.SemaphoreType.DMA((6,)),
@@ -132,7 +141,7 @@
         compiler_params=pltpu.CompilerParams(
             collective_id=0, has_side_effects=True, vmem_limit_bytes=48 * 1024 * 1024
         ),
-    )(piled)
+    )(piled, *tables)
 
 
 def shift_cycles(start_ref, g_ref, dens_ref, vrad_ref, vphi_ref, line_ref):
@@ -352,7 +361,6 @@
     cube = jax.ShapeDtypeStruct((rows, blocks, LANES), f32)
 
     piled = jnp.stack([surface_mass, outward_drift, leftover_angular_drift])
-    gathered = gather_sectors(piled.reshape(3, rows, blocks, LANES))
 
     columns = column_first + jnp.arange(sector, dtype=jnp.int32).reshape(blocks, LANES)
     cell_angles = (2 * columns + 1).astype(f32) * (jnp.pi / ANGULAR_BINS)
@@ -392,13 +400,10 @@
     th, tl = split_outside(table)
     tth, ttl = split_outside(table_t)
 
-    radial_emb, azimuthal_emb = call(
-        embryo_field,
-        (cube, cube),
-        [SMEM] * 4 + [VMEM] * 4,
-        [pltpu.VMEM((embryos, blocks, LANES), f32)] * 3,
-        flops=600_000_000,
-    )(a_table, b_table, radius, emb, cos_cell, sin_cell, half_cos, half_sin)
+    tables = (a_table, b_table, radius, emb, cos_cell, sin_cell, half_cos, half_sin)
+    gathered, radial_emb, azimuthal_emb = gather_sectors(
+        piled.reshape(3, rows, blocks, LANES), tables, embryos
+    )
 
     start = (column_first - angular_offsets) % ANGULAR_BINS
     dens_two, vrad, vphi = call(

time: 182 us -> 194 us (1.066)
  local copies, waits for them, and re-layouts: 6.18 us -> 15.7 us
  Pallas kernels: 141 us -> 134 us
  other arithmetic: 3.12 us -> 8.62 us
  starting transfers between devices: 17.1 us -> 20.1 us
    unnamed x16 -> x68, local copies, waits for them, and re-layouts: 5.76 us -> 15.3 us
    pallas_call x2 -> x1, Pallas kernels: 117 us -> 110 us  [gather_sectors(): pl.pallas_call(ring_gather, out_shape=(jax.ShapeDtypeStruct((count,) + pi...]
    ppermute x7, starting transfers between devices: 14.5 us -> 17.5 us  [butterfly(): lax.ppermute(value, axis, [(i, i ^ step) for i in range(count)])]
    ppermute x7, waiting for transfers between devices: 3 us -> 5.8 us  [butterfly(): lax.ppermute(value, axis, [(i, i ^ step) for i in range(count)])]
  transfers between devices with their start and end apart: 9 -> 9, of which waited for: 3 -> 4; matrix products, arithmetic and copies ran while one was open for 2% -> 3% of each run, Pallas kernels for 4% -> 0%
where the time goes in v3:
time: 194 us; the launch traced here: 193 us
  Pallas kernels  134 us (69%)
  starting transfers between devices  20.1 us (10%)
  local copies, waits for them, and re-layouts  15.7 us (8%)
  other arithmetic  8.62 us (4%)
  blocking collectives  8.19 us (4%)
  waiting for transfers between devices  5.81 us (3%)
    pallas_call x1, Pallas kernels, gather_sectors(): pl.pallas_call(ring_gather, out_shape=(jax.ShapeDtypeStruct((count,) + pi...  110 us
    ppermute x7, starting transfers between devices, butterfly(): lax.ppermute(value, axis, [(i, i ^ step) for i in range(count)])  17.5 us
    unnamed x68, local copies, waits for them, and re-layouts  15.3 us
    pallas_call x1, Pallas kernels, on_device(): call(embryo_push, (line, line), [SMEM] * 5 + [VMEM] * 5, [pltpu.VMEM((row...  10.2 us
    all_gather x1, blocking collectives, on_device(): every = lax.all_gather(moments, 'rad', axis=0, tiled=True)  8.19 us
    pallas_call x1, Pallas kernels, on_device(): call(shift_cycles, (cube, cube, cube), [SMEM, VMEM], [pltpu.VMEM((3, whol...  7.43 us
    ppermute x7, waiting for transfers between devices, butterfly(): lax.ppermute(value, axis, [(i, i ^ step) for i in range(count)])  5.8 us
    pallas_call x1, Pallas kernels, on_device(): call(kick, (cube, cube), [SMEM] + [VMEM] * 11, [pltpu.VMEM((rows, 2 * MOD...  4.18 us
  transfers between devices with their start and end apart: 9, of which 4 were waited for; matrix products, arithmetic and copies ran while one was open for 3% of the time, Pallas kernels for 0%

profile of v3, /device:TPU:0, one launch (start us, length us, event | category | flops | bytes accessed | tf_op | source)
XLA Modules:
  0.0 193.3 jit_solution(13221969444406496864)
XLA Ops:
  0.9 0.8 multiply_exponential_fusion
  1.9 0.7 fusion.34
  2.6 1.1 copy.13
  4.8 109.8 %shard_map.102 = (f32[4,3,32,32,128]{4,3,2,1,0:T(8,128)}, f32[32,32,128]{2,1,0:T(8,128)S(1)}, f32[32,32,128]{2,1,0:T(8,128)S(1)}) custom-call(f32[3,32,32,128]{3,2,1,0:T(8,128)S(1)} %pad_maximum_fusion.own_ref, f32[1024]{0:T(1024)S(1)} %mul.348.refs_0_.a_ref, f32[1024]{0:T(1024)S(1)} %mul.353.refs_1_.b_ref, f32[32]{0:T(128)S(1)} %get-tuple-element.62.refs_2_.r_ref, ...), custom_call_target="tpu_custom_call" | custom-call | tf_op jit(solution)/shard_map/pallas_call | solution.py:130
  114.5 7.4 %shard_map.103 = (f32[32,32,128]{2,1,0:T(8,128)S(1)}, f32[32,32,128]{2,1,0:T(8,128)S(1)}, f32[32,32,128]{2,1,0:T(8,128)S(1)}) custom-call(s32[32]{0:T(128)S(1)} %get-tuple-element.60.start_ref, f32[4,3,32,32,128]{4,3,2,1,0:T(8,128)} %get-tuple-element.16.g_ref), custom_call_target="tpu_custom_call" | custom-call | flops 10000000 | bytes 1048576 | tf_op jit(solution)/shard_map/pallas_call | solution.py:409
  122.6 1.3 collective-permute-start
  123.9 1.3 collective-permute-start.1
  127.7 0.7 fusion
  131.0 0.9 copy-done
  131.9 0.9 copy-done.1
  132.8 0.8 copy-done.19
  133.6 0.8 copy-done.21
  135.0 2.3 %shard_map.104 = (f32[32,32,128]{2,1,0:T(8,128)S(1)}, f32[32,512]{1,0:T(8,128)S(1)}) custom-call(s32[2]{0:T(128)S(1)} %copy-done.22, f32[32,32,128]{2,1,0:T(8,128)S(1)} %get-tuple-element.17.d_ref, f32[32,32,128]{2,1,0:T(8,128)S(1)} %get-tuple-element.18.v_ref.vr_ref, f32[2,1,32,128]{3,2,1,0:T(8,128)S(1)} %copy-done.19, f32[2,1,32,128]{3,2,1,0:T(8,128)S(1)} %copy-done.21, ...), custom_call_target="tpu_custom_call" | custom-call | flops 400000000 | bytes 1048576 | tf_op jit(solution)/shard_map/pallas_call | solution.py:419
  138.0 0.7 copy-done.5
  138.8 0.7 copy-done.7
  142.8 10.2 %shard_map.106 = (f32[32,128]{1,0:T(8,128)S(1)}, f32[32,128]{1,0:T(8,128)S(1)}) custom-call(f32[1024]{0:T(1024)S(1)} %copy-done.10, f32[1024]{0:T(1024)S(1)} %copy-done.12, f32[32]{0:T(128)S(1)} %copy-done.14, f32[32]{0:T(128)S(1)} %copy-done.23, f32[160]{0:T(256)S(1)} %copy-done.17, f32[32,32,128]{2,1,0:T(8,128)S(1)} %get-tuple-element.19.d_ref, ...), custom_call_target="tpu_custom_call" | custom-call | flops 600000000 | bytes 1048576 | tf_op jit(solution)/shard_map/pallas_call | solution.py:427
  153.2 2.1 %collective-permute-start.4 = (f32[2,32]{1,0:T(2,128)S(1)}, f32[2,32]{1,0:T(2,128)S(1)}, u32[]{:S(2)}, u32[]{:S(2)}) collective-permute-start(f32[2,32]{1,0:T(2,128)S(1)} %maximum_divide_fusion), channel_id=1, source_target_pairs={{0,1},{1,0},{2,3},{3,2},{4,5},{5,4},{6,7},{7,6},{8,9},{9,8},{10,11... | collective-permute-start | bytes 776 | tf_op jit(solution)/shard_map/ppermute | solution.py:330
  155.3 1.5 collective-permute-done.4
  156.9 2.9 %collective-permute-start.5 = (f32[2,32]{1,0:T(2,128)S(1)}, f32[2,32]{1,0:T(2,128)S(1)}, u32[]{:S(2)}, u32[]{:S(2)}) collective-permute-start(f32[2,32]{1,0:T(2,128)S(1)} %fusion.38), channel_id=1, source_target_pairs={{0,2},{1,3},{2,0},{3,1},{4,6},{5,7},{6,4},{7,5},{8,10},{9,11},{10,... | collective-permute-start | bytes 776 | tf_op jit(solution)/shard_map/ppermute | solution.py:330
  159.8 1.6 collective-permute-done.5
  161.4 1.1 collective-permute-start.6
  162.5 1.8 collective-permute-start.2
  164.3 3.7 %collective-permute-start.7 = (f32[2,32]{1,0:T(2,128)S(1)}, f32[2,32]{1,0:T(2,128)S(1)}, u32[]{:S(2)}, u32[]{:S(2)}) collective-permute-start(f32[2,32]{1,0:T(2,128)S(1)} %add.181), channel_id=1, source_target_pairs={{0,8},{4,12},{8,0},{12,4},{16,24},{20,28},{24,16},{28,20},{1,9},{5... | collective-permute-start | bytes 776 | tf_op jit(solution)/shard_map/ppermute | solution.py:330
  168.0 1.5 collective-permute-done.7
  169.6 3.0 %collective-permute-start.8 = (f32[2,32]{1,0:T(2,128)S(1)}, f32[2,32]{1,0:T(2,128)S(1)}, u32[]{:S(2)}, u32[]{:S(2)}) collective-permute-start(f32[2,32]{1,0:T(2,128)S(1)} %add.182), channel_id=1, source_target_pairs={{0,16},{4,20},{8,24},{12,28},{16,0},{20,4},{24,8},{28,12},{1,17},{... | collective-permute-start | bytes 776 | tf_op jit(solution)/shard_map/ppermute | solution.py:330
  172.5 3.0 %collective-permute-start.3 = (f32[32,512]{1,0:T(8,128)S(1)}, f32[32,512]{1,0:T(8,128)S(1)}, u32[]{:S(2)}, u32[]{:S(2)}) collective-permute-start(f32[32,512]{1,0:T(8,128)S(1)} %fusion.37), channel_id=1, source_target_pairs={{0,2},{1,3},{2,0},{3,1},{4,6},{5,7},{6,4},{7,5},{8,10},{9,11},{10,... | collective-permute-start | bytes 196616 | tf_op jit(solution)/shard_map/ppermute | solution.py:330
  175.7 1.1 copy.24
  177.4 1.1 collective-permute-done.3
  178.6 8.2 %all-gather.1 = f32[8,2,512]{2,1,0:T(2,128)S(1)} all-gather(f32[1,2,512]{2,1,0:T(2,128)S(1)} %maximum_bitcast_fusion), channel_id=2, replica_groups=mesh['rad'=8,'az'=4] {'rad'}, dimensions={0}, use_global_device_ids=true | all-gather | bytes 36864 | tf_op jit(solution)/shard_map/all_gather | solution.py:444
  186.9 4.2 %shard_map.105 = (f32[32,32,128]{2,1,0:T(8,128)S(1)}, f32[32,32,128]{2,1,0:T(8,128)S(1)}) custom-call(f32[32]{0:T(128)S(1)} %copy-done.15, f32[32,512]{1,0:T(8,128)S(1)} %get-tuple-element.30.x_ref, f32[2,512]{1,0:T(2,128)S(1)} %multiply_reduce_fusion.2.from_ref, f32[4,512]{1,0:T(4,128)S(1)} %copy-done.8, f32[32,256]{1,0:T(8,128)S(1)} %get-tuple-element.45.ct_ref, ...), custom_call_target="tpu_custom_call" | custom-call | flops 400000000 | bytes 1048576 | tf_op jit(solution)/shard_map/pallas_call | solution.py:458
  191.1 1.1 copy.22
  192.2 1.1 copy.23
  (106 shorter events, 13.0 us)
Async XLA Ops:
  0.6 3.1 %copy-start.24 = (f32[32,4096]{1,0:T(8,128)S(1)}, f32[32,4096]{1,0:T(8,128)}, u32[]{:S(2)}) copy-start(f32[32,4096]{1,0:T(8,128)} %param.8) | copy-start | bytes 1572868
  0.6 3.2 %copy-start.25 = (f32[32,4096]{1,0:T(8,128)S(1)}, f32[32,4096]{1,0:T(8,128)}, u32[]{:S(2)}) copy-start(f32[32,4096]{1,0:T(8,128)} %param.9) | copy-start | bytes 1572868
  0.7 4.0 %copy-start.2 = (f32[32,128]{1,0:T(8,128)}, f32[32,128]{1,0:T(8,128)S(1)}, u32[]{:S(2)}) copy-start(f32[32,128]{1,0:T(8,128)S(1)} %get-tuple-element.57.refs_4_.cos_ref) | copy-start | bytes 49156
  0.8 3.9 %copy-start.4 = (f32[32,128]{1,0:T(8,128)}, f32[32,128]{1,0:T(8,128)S(1)}, u32[]{:S(2)}) copy-start(f32[32,128]{1,0:T(8,128)S(1)} %get-tuple-element.58.refs_7_.hs_ref) | copy-start | bytes 49156
  0.9 3.9 %copy-start.6 = (f32[32,128]{1,0:T(8,128)}, f32[32,128]{1,0:T(8,128)S(1)}, u32[]{:S(2)}) copy-start(f32[32,128]{1,0:T(8,128)S(1)} %get-tuple-element.59.refs_6_.hc_ref) | copy-start | bytes 49156
  0.9 3.9 %copy-start.13 = (f32[32]{0:T(128)}, f32[32]{0:T(128)S(1)}, u32[]{:S(2)}) copy-start(f32[32]{0:T(128)S(1)} %get-tuple-element.62.refs_2_.r_ref) | copy-start | bytes 388
  1.8 2.9 %copy-start.9 = (f32[1024]{0:T(1024)}, f32[1024]{0:T(1024)S(1)}, u32[]{:S(2)}) copy-start(f32[1024]{0:T(1024)S(1)} %mul.348.refs_0_.a_ref) | copy-start | bytes 12292
  1.9 2.9 %copy-start.11 = (f32[1024]{0:T(1024)}, f32[1024]{0:T(1024)S(1)}, u32[]{:S(2)}) copy-start(f32[1024]{0:T(1024)S(1)} %mul.353.refs_1_.b_ref) | copy-start | bytes 12292
  2.6 1.4 copy-start.30
  4.7 117.2 %copy-start.16 = (f32[160]{0:T(256)}, f32[160]{0:T(256)S(1)}, u32[]{:S(2)}) copy-start(f32[160]{0:T(256)S(1)} %concatenate.65.refs_3_.emb_ref) | copy-start | bytes 1924
  122.0 4.9 %copy-start.29 = (s32[32]{0:T(128)S(1)}, s32[32]{0:T(128)}, u32[]{:S(2)}) copy-start(s32[32]{0:T(128)} %get-tuple-element.61) | copy-start | bytes 388
  122.6 7.2 %collective-permute-start = (f32[2,1,32,128]{3,2,1,0:T(8,128)}, f32[2,1,32,128]{3,2,1,0:T(8,128)S(1)}, u32[]{:S(2)}, u32[]{:S(2)}) collective-permute-start(f32[2,1,32,128]{3,2,1,0:T(8,128)} %get-tuple-element.32), channel_id=1, source_target_pairs={{0,4},{4,8},{8,12},{12,16},{16,20},{20,24},{24,28},{1,5},{5,9},{9,... | collective-permute-start | bytes 98312 | tf_op jit(solution)/shard_map/ppermute | solution.py:338
  123.9 6.5 %collective-permute-start.1 = (f32[2,1,32,128]{3,2,1,0:T(8,128)}, f32[2,1,32,128]{3,2,1,0:T(8,128)S(1)}, u32[]{:S(2)}, u32[]{:S(2)}) collective-permute-start(f32[2,1,32,128]{3,2,1,0:T(8,128)} %get-tuple-element.31), channel_id=1, source_target_pairs={{4,0},{8,4},{12,8},{16,12},{20,16},{24,20},{28,24},{5,1},{9,5},{13... | collective-permute-start | bytes 98312 | tf_op jit(solution)/shard_map/ppermute | solution.py:339
  131.0 0.9 copy-start
  131.9 0.9 copy-start.1
  132.8 0.8 copy-start.19
  133.6 0.8 copy-start.21
  137.3 15.9 %copy-start.28 = (f32[32]{0:T(128)S(1)}, f32[32]{0:T(128)}, u32[]{:S(2)}) copy-start(f32[32]{0:T(128)} %param.13) | copy-start | bytes 388
  137.3 0.7 copy-start.3
  138.0 0.7 copy-start.5
  138.8 0.7 copy-start.7
  142.7 35.7 %copy-start.26 = (f32[512]{0:T(512)S(1)}, f32[512]{0:T(512)}, u32[]{:S(2)}) copy-start(f32[512]{0:T(512)} %get-tuple-element.39) | copy-start | bytes 6148
  142.8 44.0 %copy-start.27 = (f32[512]{0:T(512)S(1)}, f32[512]{0:T(512)}, u32[]{:S(2)}) copy-start(f32[512]{0:T(512)} %get-tuple-element.38) | copy-start | bytes 6148
  142.8 44.1 %copy-start.8 = (f32[4,512]{1,0:T(4,128)S(1)}, f32[4,512]{1,0:T(4,128)}, u32[]{:S(2)}) copy-start(f32[4,512]{1,0:T(4,128)} %pad_maximum_fusion.5.rate_ref) | copy-start | bytes 24580
  142.8 44.1 %copy-start.15 = (f32[32]{0:T(128)S(1)}, f32[32]{0:T(128)}, u32[]{:S(2)}) copy-start(f32[32]{0:T(128)} %copy-done.13) | copy-start | bytes 388
  153.2 3.6 %collective-permute-start.4 = (f32[2,32]{1,0:T(2,128)S(1)}, f32[2,32]{1,0:T(2,128)S(1)}, u32[]{:S(2)}, u32[]{:S(2)}) collective-permute-start(f32[2,32]{1,0:T(2,128)S(1)} %maximum_divide_fusion), channel_id=1, source_target_pairs={{0,1},{1,0},{2,3},{3,2},{4,5},{5,4},{6,7},{7,6},{8,9},{9,8},{10,11... | collective-permute-start | bytes 776 | tf_op jit(solution)/shard_map/ppermute | solution.py:330
  156.9 4.5 %collective-permute-start.5 = (f32[2,32]{1,0:T(2,128)S(1)}, f32[2,32]{1,0:T(2,128)S(1)}, u32[]{:S(2)}, u32[]{:S(2)}) collective-permute-start(f32[2,32]{1,0:T(2,128)S(1)} %fusion.38), channel_id=1, source_target_pairs={{0,2},{1,3},{2,0},{3,1},{4,6},{5,7},{6,4},{7,5},{8,10},{9,11},{10,... | collective-permute-start | bytes 776 | tf_op jit(solution)/shard_map/ppermute | solution.py:330
  161.4 2.9 %collective-permute-start.6 = (f32[2,32]{1,0:T(2,128)S(1)}, f32[2,32]{1,0:T(2,128)S(1)}, u32[]{:S(2)}, u32[]{:S(2)}) collective-permute-start(f32[2,32]{1,0:T(2,128)S(1)} %fusion.39), channel_id=1, source_target_pairs={{0,4},{4,0},{8,12},{12,8},{16,20},{20,16},{24,28},{28,24},{1,5},{5... | collective-permute-start | bytes 776 | tf_op jit(solution)/shard_map/ppermute | solution.py:330
  162.5 10.0 %collective-permute-start.2 = (f32[32,512]{1,0:T(8,128)S(1)}, f32[32,512]{1,0:T(8,128)S(1)}, u32[]{:S(2)}, u32[]{:S(2)}) collective-permute-start(f32[32,512]{1,0:T(8,128)S(1)} %broadcast_multiply_fusion), channel_id=1, source_target_pairs={{0,1},{1,0},{2,3},{3,2},{4,5},{5,4},{6,7},{7,6},{8,9},{9,8},{10,11... | collective-permute-start | bytes 196616 | tf_op jit(solution)/shard_map/ppermute | solution.py:330
  164.3 5.2 %collective-permute-start.7 = (f32[2,32]{1,0:T(2,128)S(1)}, f32[2,32]{1,0:T(2,128)S(1)}, u32[]{:S(2)}, u32[]{:S(2)}) collective-permute-start(f32[2,32]{1,0:T(2,128)S(1)} %add.181), channel_id=1, source_target_pairs={{0,8},{4,12},{8,0},{12,4},{16,24},{20,28},{24,16},{28,20},{1,9},{5... | collective-permute-start | bytes 776 | tf_op jit(solution)/shard_map/ppermute | solution.py:330
  169.6 7.3 %collective-permute-start.8 = (f32[2,32]{1,0:T(2,128)S(1)}, f32[2,32]{1,0:T(2,128)S(1)}, u32[]{:S(2)}, u32[]{:S(2)}) collective-permute-start(f32[2,32]{1,0:T(2,128)S(1)} %add.182), channel_id=1, source_target_pairs={{0,16},{4,20},{8,24},{12,28},{16,0},{20,4},{24,8},{28,12},{1,17},{... | collective-permute-start | bytes 776 | tf_op jit(solution)/shard_map/ppermute | solution.py:330
  172.5 5.9 %collective-permute-start.3 = (f32[32,512]{1,0:T(8,128)S(1)}, f32[32,512]{1,0:T(8,128)S(1)}, u32[]{:S(2)}, u32[]{:S(2)}) collective-permute-start(f32[32,512]{1,0:T(8,128)S(1)} %fusion.37), channel_id=1, source_target_pairs={{0,2},{1,3},{2,0},{3,1},{4,6},{5,7},{6,4},{7,5},{8,10},{9,11},{10,... | collective-permute-start | bytes 196616 | tf_op jit(solution)/shard_map/ppermute | solution.py:330
  (8 other events, 5.2 us)
